TPU v7x, 32 devices: a whole 2x2x4 slice. The times are simulated.
32 devices in a mesh: dp: 4 (over z), row: 4 (over y, x), col: 2 (over core).
Axes of the slice: x: 2, y: 2, z: 4, core: 2. Of those that a mesh axis runs over, the one named last changes fastest.
Arguments:
- tokens: bfloat16 [2048, 1024], P('dp', ('row', 'col')), may hold values from -7.5 to 7.5
- out_grad: bfloat16 [2048, 1024], P('dp', ('row', 'col')), may hold values from -6 to 6
- doc_ids: int32 [2048], P('dp'), may hold values from 0 to 3, never falling along the last dimension, each value on 1 to 1024 neighbouring positions
- expert_ids: int32 [2048, 8], P('dp'), may hold values from 0 to 31, all different within a row
- gain_attn: bfloat16 [1024], P(('row', 'col')), may hold values from 0.5 to 1.5
- w_query: bfloat16 [1024, 1024], P(None, ('row', 'col')), may hold values from -1.1015625 to 1.1015625
- w_key_value: bfloat16 [1024, 8, 128], P(None, ('row', 'col')), may hold values from -0.1875 to 0.1875
- w_output: bfloat16 [1024, 1024], P(('row', 'col')), may hold values from -6 to 6
- gain_moe: bfloat16 [1024], P(('row', 'col')), may hold values from 0.5 to 1.5
- w_router: bfloat16 [1024, 32], P(('row', 'col')), may hold values from -2.75 to 2.75
- w_expert_in: bfloat16 [32, 1024, 2, 512], P('row', None, None, 'col'), may hold values from -0.1875 to 0.1875
- w_expert_out: bfloat16 [32, 512, 1024], P('row', 'col'), may hold values from -4 to 4
Outputs:
- block_out: bfloat16 [2048, 1024], P('dp', ('row', 'col'))
- in_grad: bfloat16 [2048, 1024], P('dp', ('row', 'col'))
- grad_gain_attn: float32 [1024], P(('row', 'col'))
- grad_query: float32 [1024, 1024], P(None, ('row', 'col'))
- grad_key_value: float32 [1024, 8, 128], P(None, ('row', 'col'))
- grad_output: float32 [1024, 1024], P(('row', 'col'))
- grad_gain_moe: float32 [1024], P(('row', 'col'))
- grad_router: float32 [1024, 32], P(('row', 'col'))
- grad_expert_in: float32 [32, 1024, 2, 512], P('row', None, None, 'col')
- grad_expert_out: float32 [32, 512, 1024], P('row', 'col')
Inputs may be any that keep to these rules, and one draw needn't show every extreme that they name: `doc_ids`: never falling along the token stream; every document has 1 to 1024 tokens and one has exactly 1024. `expert_ids`: each row names 8 different experts; every expert is named by some row.
All inputs are finite; a program needn't handle non-finite values.
Results may differ from a plain program's by a relative error of at most 0.02555.
Values may be sent and summed in bfloat16 or wider, within the bound.
A program may use at most 192 MiB of HBM per device.

v0:
```python
import functools

import jax
import jax.numpy as jnp
from jax import lax
from jax.experimental import pallas as pl
from jax.experimental.pallas import tpu as pltpu
from jax.sharding import PartitionSpec as P

LONGEST = 4096
HIGH = lax.Precision.HIGHEST
EPSILON = 1e-05
RESIDUAL_SCALE = 0.22
SCORE_SCALE = 0.015625
ROPE_BASE = 10000.0
MASKED = -1e30
MESH = pl.DeviceIdType.MESH
GROUP = ("row", "col")
EVERY = ("dp", "row", "col")
LANES = 128
HBM = pl.BlockSpec(memory_space=pl.ANY)
FULL = pl.BlockSpec(memory_space=pltpu.VMEM)
TURN = LANES // 4


class Moves:
    def __init__(self, sizes, kinds, sources, targets, sems):
        self.sizes, self.kinds = sizes, kinds
        self.sources, self.targets = sources, targets
        self.send_sem, self.recv_sem, self.local_sem = sems

    def place(self):
        row, col, layer = lax.axis_index("row"), lax.axis_index("col"), lax.axis_index("dp")
        return row, col, layer, row * self.sizes[1] + col

    def member(self, index):
        rows, cols, depth = self.sizes
        return {"row": index // cols, "col": lax.rem(index, cols)}

    def barrier(self):
        rows, cols, depth = self.sizes
        row, col, layer, me = self.place()
        group = rows * cols
        names = [kind[0] for kind in self.kinds]
        barrier = pltpu.get_barrier_semaphore()
        partners = []
        if "swap" in names:
            for k in range(1, group):
                partners.append(self.member(lax.rem(me + k, group)))
        elif "gather" in names:
            for k in range(1, rows):
                partners.append({"row": lax.rem(row + k, rows)})
            for k in range(1, cols):
                partners.append({"col": lax.rem(col + k, cols)})
        shifts = set()
        for kind in self.kinds:
            if kind[0] == "shift":
                for d in kind[1]:
                    shifts |= {d % depth, -d % depth}
            elif kind[0] in ("turn", "collect"):
                shifts |= set(range(1, depth))
        for k in sorted(shifts - {0}):
            partners.append({"dp": lax.rem(layer + k, depth)})
        for partner in partners:
            pl.semaphore_signal(barrier, inc=1, device_id=partner, device_id_type=MESH)
        pl.semaphore_wait(barrier, len(partners))

    def copies(self, only):
        rows, cols, depth = self.sizes
        row, col, layer, me = self.place()
        group = rows * cols
        slot = 0
        lists = []

        def remote(source, target, device):
            nonlocal slot
            slot += 1
            return functools.partial(
                pltpu.make_async_remote_copy,
                src_ref=source,
                dst_ref=target,
                send_sem=self.send_sem.at[slot - 1],
                recv_sem=self.recv_sem.at[slot - 1],
                device_id=device,
                device_id_type=MESH,
            )

        for index, (kind, source, target) in enumerate(
            zip(self.kinds, self.sources, self.targets)
        ):
            direct, relayed, local = [], [], []

            def keep(source, target):
                sem = self.local_sem.at[index]
                local.append(functools.partial(pltpu.make_async_copy, source, target, sem))

            if kind[0] == "gather":
                second, parts = kind[1:]
                size = source.shape[0] // parts

                def at(i, part):
                    some = pl.ds(part * size, size)
                    return target.at[some, i] if second else target.at[i, some]

                for part in range(parts):
                    some = source.at[pl.ds(part * size, size)]
                    for k in range(1, rows):
                        device = {"row": lax.rem(row + k, rows)}
                        copy = remote(some, at(me, part), device)
                        piece = at(lax.rem(row + rows - k, rows) * cols + col, part)
                        nexts = [
                            remote(piece, piece, {"col": lax.rem(col + j, cols)})
                            for j in range(1, cols)
                        ]
                        relayed.append((copy, nexts))
                    for k in range(1, cols):
                        device = {"col": lax.rem(col + k, cols)}
                        direct.append(remote(some, at(me, part), device))
                keep(source, target.at[:, me] if second else target.at[me])
            elif kind[0] == "swap":
                for k in range(1, group):
                    other = lax.rem(me + k, group)
                    direct.append(remote(source.at[other], target.at[me], self.member(other)))
                keep(source.at[me], target.at[me])
            elif kind[0] in ("turn", "collect"):
                for k in range(1, depth):
                    other = lax.rem(layer + k, depth)
                    piece = source.at[other] if kind[0] == "turn" else source
                    direct.append(remote(piece, target.at[layer], {"dp": other}))
                keep(source.at[layer] if kind[0] == "turn" else source, target.at[layer])
            else:
                for at, d in enumerate(kind[1]):
                    piece = source.at[at] if kind[2] else source
                    device = {"dp": lax.rem(layer + d % depth, depth)}
                    direct.append(remote(piece, target.at[at], device))
            if only is None or index in only:
                lists.append((direct, relayed, local))
        return tuple(sum((part[i] for part in lists), []) for i in range(3))

    def start(self, only=None):
        direct, relayed, local = self.copies(only)
        for copy, _ in relayed:
            copy().start()
        for copy in direct + local:
            copy().start()

    def relay(self, only=None):
        for copy, nexts in self.copies(only)[1]:
            copy().wait_recv()
            for follower in nexts:
                follower().start()

    def finish(self, only=None):
        direct, relayed, local = self.copies(only)
        for copy, nexts in relayed:
            copy().wait_send()
            for follower in nexts:
                follower().wait()
        for copy in direct + local:
            copy().wait()


def planned(sizes, items):
    rows, cols, depth = sizes
    group = rows * cols
    kinds, shapes, copies = [], [], 0
    for item in items:
        name, array = item[0], item[1]
        shape = array.shape
        if name == "gather":
            second, parts = (item[2:] + (False, 1)[len(item) - 2 :])[:2]
            kinds.append((name, second, parts))
            shape = (shape[0], group) + shape[1:] if second else (group,) + shape
            copies += parts * ((rows - 1) * cols + cols - 1)
        elif name == "shift":
            distances, split = item[2], item[3]
            kinds.append((name, tuple(distances), split))
            shape = (len(distances),) + (shape[1:] if split else shape)
            copies += len(distances)
        else:
            kinds.append((name,))
            if name == "collect":
                shape = (depth,) + shape
            copies += (group if name == "swap" else depth) - 1
        shapes.append(jax.ShapeDtypeStruct(shape, array.dtype))
    sems = [
        pltpu.SemaphoreType.DMA((copies,)),
        pltpu.SemaphoreType.DMA((copies,)),
        pltpu.SemaphoreType.DMA((len(items),)),
    ]
    return tuple(kinds), shapes, sems


def exchange_body(sizes, kinds, *refs):
    count = len(kinds)
    moves = Moves(sizes, kinds, refs[:count], refs[count : 2 * count], refs[2 * count :])
    moves.barrier()
    moves.start()
    moves.relay()
    moves.finish()


def exchange(sizes, name, number, *items):
    kinds, shapes, sems = planned(sizes, items)
    return pl.pallas_call(
        functools.partial(exchange_body, sizes, kinds),
        out_shape=tuple(shapes),
        in_specs=[HBM] * len(items),
        out_specs=(HBM,) * len(items),
        scratch_shapes=sems,
        compiler_params=pltpu.CompilerParams(collective_id=number, has_side_effects=True),
        name=name,
    )(*[item[1] for item in items])


def dot(a, b, left=1, right=0, precision=None):
    return lax.dot_general(
        a,
        b,
        (((left,), (right,)), ((), ())),
        preferred_element_type=jnp.float32,
        precision=precision,
    )


def call(body, name, shapes, *arrays, scratch=()):
    return pl.pallas_call(
        body,
        out_shape=tuple(jax.ShapeDtypeStruct(*shape) for shape in shapes),
        in_specs=[FULL] * len(arrays),
        out_specs=(FULL,) * len(shapes),
        scratch_shapes=list(scratch),
        name=name,
    )(*arrays)


def hosted(body, name, shapes, *arrays, scratch=(), sizes, number, items):
    kinds, moved, sems = planned(sizes, items)
    ins, count, outs = len(arrays), len(items), len(shapes)

    def whole(*refs):
        sources = refs[ins : ins + count]
        made = refs[ins + count : ins + count + outs]
        targets = refs[ins + count + outs : ins + 2 * count + outs]
        rest = refs[ins + 2 * count + outs :]
        moves = Moves(sizes, kinds, sources, targets, rest[len(scratch) :])
        moves.barrier()
        moves.start()
        body(*refs[:ins], *made, *rest[: len(scratch)])
        moves.relay()
        moves.finish()

    return pl.pallas_call(
        whole,
        out_shape=tuple(jax.ShapeDtypeStruct(*shape) for shape in shapes) + tuple(moved),
        in_specs=[FULL] * ins + [HBM] * count,
        out_specs=(FULL,) * outs + (HBM,) * count,
        scratch_shapes=list(scratch) + sems,
        compiler_params=pltpu.CompilerParams(collective_id=number, has_side_effects=True),
        name=name,
    )(*arrays, *[item[1] for item in items])


def lanes_of(shape):
    return lax.broadcasted_iota(jnp.int32, shape, len(shape) - 1)


def flipped(values):
    lanes = lanes_of(values.shape)
    ahead = pltpu.roll(values, LANES - TURN, 1)
    behind = pltpu.roll(values, TURN, 1)
    return jnp.where(lanes % (2 * TURN) < TURN, ahead, behind)


def beside(blocks_ref):
    return jnp.concatenate([blocks_ref[i] for i in range(blocks_ref.shape[0])], axis=1)


def gain_row(gains_ref, which):
    return beside(gains_ref).astype(jnp.float32)[which : which + 1, :]


def added(blocks):
    return functools.reduce(
        jnp.add, [blocks[i].astype(jnp.float32) for i in range(blocks.shape[0])]
    )


def own_rows(count):
    me = lax.axis_index("row") * lax.axis_size("col") + lax.axis_index("col")
    return pl.ds(pl.multiple_of(me * count, count), count)


def column(row):
    return jnp.broadcast_to(row, (8, row.shape[1])).T[:, 0:1]


def project_body(blocks, gains, w_query, w_pair, cosine, sine, near, far, normed, query, pair, own, own_grad, near_turned, far_turned):
    tokens = beside(blocks).astype(jnp.float32)
    scale = lax.rsqrt(jnp.mean(tokens * tokens, axis=1, keepdims=True) + EPSILON)
    normed[...] = (tokens * scale * gain_row(gains, 0)).astype(jnp.bfloat16)
    raw = dot(normed[...], w_query[...])
    query[...] = (raw * cosine[...] + flipped(raw) * sine[...]).astype(jnp.bfloat16)
    raw = dot(normed[...], w_pair[...])
    keys = lanes_of(raw.shape) < LANES // 2
    turned = raw * cosine[...] + flipped(raw) * sine[...]
    pair[...] = jnp.where(keys, turned, raw).astype(jnp.bfloat16)
    for i in range(blocks.shape[0]):
        own[:, i * LANES : (i + 1) * LANES] = blocks[i, own_rows(own.shape[0]), :]
    for source, target in ((near, near_turned), (far, far_turned)):
        for i in range(source.shape[0]):
            scaled = RESIDUAL_SCALE * source[i].astype(jnp.float32)
            target[i] = scaled.T.astype(jnp.bfloat16)
    for i in range(near.shape[0]):
        own_grad[:, i * LANES : (i + 1) * LANES] = near[i, own_rows(own.shape[0]), :]


def doubled(pair, keys_ref, values_ref, at):
    wide = pair.astype(jnp.float32)
    other = pltpu.roll(wide, LANES // 2, 1)
    keys = lanes_of(wide.shape) < LANES // 2
    keys_ref[at] = jnp.where(keys, wide, other).astype(jnp.bfloat16)
    values_ref[at] = jnp.where(keys, other, wide).astype(jnp.bfloat16)


def per_head(values):
    first = lanes_of(values.shape) < LANES // 2
    zero = jnp.zeros_like(values)
    return jnp.concatenate(
        [jnp.where(first, values, zero), jnp.where(first, zero, values)], axis=0
    )


def tile_scores(queries, keys_ref, starts, row, block, last, tokens):
    scores = dot(queries, keys_ref[block], 1, 1) * SCORE_SCALE
    at = lanes_of(scores.shape) + block * tokens
    allowed = at >= starts
    if block == last:
        place = row + lax.broadcasted_iota(jnp.int32, scores.shape, 0)
        allowed = allowed & (at <= place + block * tokens)
    return jnp.where(allowed, scores, MASKED)


def doc_row(docs):
    rows = [docs[i : i + 1, :] for i in range(docs.shape[0])]
    return jnp.concatenate(rows, axis=1).astype(jnp.float32)


def attend_body(query, pair, far, docs, far_docs, mixed, log_total, start, keys, values, queries, out):
    tokens = query.shape[0]
    last = far.shape[0]
    layer = lax.axis_index("dp")
    here = doc_row(docs[...])
    mine = column(here)
    before = jnp.sum((here < mine).astype(jnp.float32), axis=1, keepdims=True)
    for d in range(1, last + 1):
        fewer = (doc_row(far_docs[d - 1]) < mine) | (layer < d)
        before = before + jnp.sum(fewer.astype(jnp.float32), axis=1, keepdims=True)
    start[...] = before.astype(jnp.int32)
    doubled(pair[...], keys, values, last)
    for d in range(1, last + 1):
        doubled(far[d - 1], keys, values, last - d)
    queries[...] = per_head(query[...].astype(jnp.float32)).astype(jnp.bfloat16)
    step = 256

    def tile(i, carry):
        rows = pl.ds(pl.multiple_of(i * step, step), step)
        row = lax.rem(i * step, tokens)
        starts = start[pl.ds(pl.multiple_of(row, step), step), :]
        parts = [
            tile_scores(queries[rows, :], keys, starts, row, block, last, tokens)
            for block in range(last + 1)
        ]
        top = functools.reduce(
            jnp.maximum, [jnp.max(part, axis=1, keepdims=True) for part in parts]
        )
        parts = [jnp.exp(part - top) for part in parts]
        total = functools.reduce(jnp.add, [jnp.sum(p, axis=1, keepdims=True) for p in parts])
        sums = [
            dot(part.astype(jnp.bfloat16), values[block]) for block, part in enumerate(parts)
        ]
        out[rows, :] = functools.reduce(jnp.add, sums) / total
        log_total[rows, :] = top + jnp.log(total)
        return carry

    lax.fori_loop(0, 2 * tokens // step, tile, 0)
    first = lanes_of((tokens, LANES)) < LANES // 2
    mixed[...] = jnp.where(first, out[:tokens, :], out[tokens:, :]).astype(jnp.bfloat16)


def attend_back_body(grad, w_output, query, pair, far, start, log_total, mixed, cosine, sine, query_grad, pair_grad, far_grad, output_grad, keys, values, queries, grads, turned, key_sums, value_sums):
    tokens = query.shape[0]
    last = far.shape[0]
    doubled(pair[...], keys, values, last)
    for d in range(1, last + 1):
        doubled(far[d - 1], keys, values, last - d)
    queries[...] = per_head(query[...].astype(jnp.float32)).astype(jnp.bfloat16)
    grads[...] = per_head(dot(grad[...], w_output[...], 1, 1)).astype(jnp.bfloat16)
    output_sum = dot(mixed[...], grad[...], 0, 0).astype(jnp.bfloat16)
    for i in range(output_grad.shape[0]):
        output_grad[i] = output_sum[:, i * LANES : (i + 1) * LANES]
    key_sums[...] = jnp.zeros_like(key_sums)
    value_sums[...] = jnp.zeros_like(value_sums)
    step = 256

    def tile(i, carry):
        rows = pl.ds(pl.multiple_of(i * step, step), step)
        row = lax.rem(i * step, tokens)
        starts = start[pl.ds(pl.multiple_of(row, step), step), :]
        asked, given, level = queries[rows, :], grads[rows, :], log_total[rows, :]
        chances, products = [], []
        for block in range(last + 1):
            scores = tile_scores(asked, keys, starts, row, block, last, tokens)
            chances.append(jnp.exp(scores - level))
            products.append(dot(given, values[block], 1, 1))
        delta = functools.reduce(
            jnp.add,
            [jnp.sum(p * q, axis=1, keepdims=True) for p, q in zip(chances, products)],
        )
        total = jnp.zeros((step, LANES), jnp.float32)
        for block in range(last + 1):
            back = (chances[block] * (products[block] - delta)).astype(jnp.bfloat16)
            total = total + dot(back, keys[block])
            key_sums[block] += dot(back, asked, 0, 0)
            value_sums[block] += dot(chances[block].astype(jnp.bfloat16), given, 0, 0)
        turned[rows, :] = total
        return carry

    lax.fori_loop(0, 2 * tokens // step, tile, 0)
    first = lanes_of((tokens, LANES)) < LANES // 2
    raw = jnp.where(first, turned[:tokens, :], turned[tokens:, :]) * SCORE_SCALE
    query_grad[...] = (raw * cosine[...] - flipped(raw) * sine[...]).astype(jnp.bfloat16)

    def joined(block):
        by_key, by_value = key_sums[block], value_sums[block]
        by_key = (by_key + pltpu.roll(by_key, LANES // 2, 1)) * SCORE_SCALE
        by_value = by_value + pltpu.roll(by_value, LANES // 2, 1)
        return jnp.where(first, by_key, by_value)

    pair_grad[...] = joined(last)
    for d in range(1, last + 1):
        far_grad[d - 1] = joined(last - d).astype(jnp.bfloat16)


def router_rows(router):
    rows = beside(router).astype(jnp.float32)
    blank = jnp.zeros((LANES - rows.shape[0], rows.shape[1]), jnp.float32)
    return jnp.concatenate([rows, blank], axis=0)


def middle_body(mixed, own, w_output, gains, router, ids_turned, rows, middle, weights, ids_ref):
    experts = router.shape[1]
    width = own.shape[1]
    attn = dot(beside(mixed), w_output[...])
    value = own[...].astype(jnp.float32) + RESIDUAL_SCALE * attn
    middle[...] = value
    scale = lax.rsqrt(jnp.mean(value * value, axis=1, keepdims=True) + EPSILON)
    normed = value * scale * gain_row(gains, 1)
    logits = dot(normed, router_rows(router), 1, 1, precision=HIGH)
    count = own.shape[0]
    ids_ref[...] = ids_turned[...].astype(jnp.float32).T
    ids = ids_ref[own_rows(count), :]
    lanes = lanes_of((count, LANES))
    chosen = jnp.zeros((count, LANES), jnp.float32)
    for k in range(ids.shape[1]):
        chosen = chosen + (ids[:, k : k + 1] == lanes.astype(jnp.float32)).astype(
            jnp.float32
        )
    top = jnp.max(jnp.where(lanes < experts, logits, MASKED), axis=1, keepdims=True)
    terms = jnp.exp(jnp.minimum(logits - top, 0.0)) * chosen
    share = terms / jnp.sum(terms, axis=1, keepdims=True)
    weights[...] = share
    high = share.astype(jnp.bfloat16)
    low = share - high.astype(jnp.float32)
    rows[:, :width] = normed.astype(jnp.bfloat16)
    rows[:, width:] = (high.astype(jnp.float32) + pltpu.roll(low, LANES // 2, 1)).astype(
        jnp.bfloat16
    )


def middle_back_body(back, out_grad, middle, weights, gains, router, middle_grad, attn_grad, logit_grad, gain_part):
    width = middle.shape[1]
    normed_grad = back[0, :, :width].astype(jnp.float32)
    weight_grad = back[0, :, width:].astype(jnp.float32)
    for i in range(1, back.shape[0]):
        normed_grad = normed_grad + back[i, :, :width].astype(jnp.float32)
        weight_grad = weight_grad + back[i, :, width:].astype(jnp.float32)
    share, value = weights[...], middle[...]
    mean = jnp.sum(share * weight_grad, axis=1, keepdims=True)
    logit = share * (weight_grad - mean)
    logit_grad[...] = logit.astype(jnp.bfloat16)
    normed_grad = normed_grad + dot(logit, router_rows(router), precision=HIGH)
    scale = lax.rsqrt(jnp.mean(value * value, axis=1, keepdims=True) + EPSILON)
    gain_part[...] = jnp.sum(normed_grad * value * scale, axis=0, keepdims=True)
    scaled = normed_grad * gain_row(gains, 1)
    norm_dot = jnp.sum(scaled * value, axis=1, keepdims=True)
    total = (
        out_grad[...].astype(jnp.float32)
        + scale * scaled
        - value * (scale * scale * scale * norm_dot / width)
    )
    middle_grad[...] = total
    attn_grad[...] = (RESIDUAL_SCALE * total).astype(jnp.bfloat16)


def project_back_body(query_grad, pair_grad, returned, normed, w_query, w_pair, cosine, sine, output_turned, logit, rows, gains, gain_moe, partial, sums, output_summed, gain_parts):
    layer = lax.axis_index("dp")
    depth = lax.axis_size("dp")
    total = pair_grad[...]
    for i in range(returned.shape[0]):
        total = total + jnp.where(
            layer + i + 1 < depth, returned[i].astype(jnp.float32), 0.0
        )
    keys = lanes_of(total.shape) < LANES // 2
    turned = total * cosine[...] - flipped(total) * sine[...]
    pair_low = jnp.where(keys, turned, total).astype(jnp.bfloat16)
    query_low = query_grad[...]
    whole = dot(query_low, w_query[...], 1, 1) + dot(pair_low, w_pair[...], 1, 1)
    partial[...] = whole.astype(jnp.bfloat16)
    gain_attn = jnp.sum(whole * normed[...].astype(jnp.float32), axis=0, keepdims=True)
    gain_attn = gain_attn / gain_row(gains, 0)
    gain_parts[...] = jnp.zeros_like(gain_parts)
    for i in range(gain_parts.shape[0]):
        at = slice(i * LANES, (i + 1) * LANES)
        gain_parts[i, 0:1, :] = gain_attn[:, at]
        gain_parts[i, 1:2, :] = gain_moe[0:1, at]
    width = normed.shape[1]
    sums[:width, :] = dot(normed[...], query_low, 0, 0).astype(jnp.bfloat16)
    sums[width : 2 * width, :] = dot(normed[...], pair_low, 0, 0).astype(jnp.bfloat16)
    output_summed[...] = added(output_turned).astype(jnp.bfloat16)
    mine = rows[:, own_rows(LANES)]
    sums[2 * width : 2 * width + LANES, :] = dot(logit[...], mine, 0, 0).astype(jnp.bfloat16)


def results_body(blocks, moe, own, middle, middle_grad, gains, gain_blocks, turned, block_out, in_grad, gain_sum, summed):
    gain_sum[...] = added(gain_blocks)
    summed[...] = added(turned).astype(jnp.bfloat16)
    width = own.shape[1]
    normed_grad = blocks[0].astype(jnp.float32)
    branch = moe[0].astype(jnp.float32)
    for i in range(1, blocks.shape[0]):
        normed_grad = normed_grad + blocks[i].astype(jnp.float32)
        branch = branch + moe[i].astype(jnp.float32)
    value = own[...].astype(jnp.float32)
    scale = lax.rsqrt(jnp.mean(value * value, axis=1, keepdims=True) + EPSILON)
    scaled = normed_grad * gain_row(gains, 0)
    norm_dot = jnp.sum(scaled * value, axis=1, keepdims=True)
    grad = (
        middle_grad[...] + scale * scaled - value * (scale * scale * scale * norm_dot / width)
    ).astype(jnp.bfloat16)
    out = (middle[...] + RESIDUAL_SCALE * branch).astype(jnp.bfloat16)
    for i in range(block_out.shape[0]):
        at = slice(i * LANES, (i + 1) * LANES)
        block_out[i] = out[:, at]
        in_grad[i] = grad[:, at]


def expert_terms(gate_up, active_grad, weight):
    hidden = active_grad.shape[0]
    gate, up = gate_up[:hidden], gate_up[hidden:]
    sigmoid = jax.nn.sigmoid(gate)
    silu = gate * sigmoid
    ungated = silu * up
    active = (ungated * weight).astype(jnp.bfloat16)
    scaled = active_grad * weight
    gate_grad = (scaled * up * sigmoid * (1.0 + gate * (1.0 - sigmoid))).astype(jnp.bfloat16)
    up_grad = (scaled * silu).astype(jnp.bfloat16)
    return active, jnp.concatenate([gate_grad, up_grad], axis=0), active_grad * ungated


def weight_rows(extra):
    turned = extra.astype(jnp.float32).T
    return turned[: LANES // 2] + turned[LANES // 2 :]


def local_experts_body(sizes, kinds, rows_ref, grads_ref, in_ref, out_ref, sent_grads, sent_rows, moe_ref, back_ref, flat_ref, in_sum, out_sum, got_grads, got_rows, moe_acc, back_acc, share, weights, spread, *sems):
    step, steps = pl.program_id(0), pl.num_programs(0)
    each, hidden, width = out_ref.shape
    parts = hidden // LANES
    moves = Moves(sizes, kinds, [sent_grads, sent_rows], [got_grads, got_rows], sems)

    @pl.when(step == 0)
    def _():
        moves.barrier()
        moves.start()
        moe_acc[...] = jnp.zeros_like(moe_acc)
        back_acc[...] = jnp.zeros_like(back_acc)
        share[...] = jnp.zeros_like(share)
        weights[...] = weight_rows(rows_ref[:, width:])

    @pl.when(step == steps // 2)
    def _():
        moves.relay([0])

    for i in range(each):
        spread[i] = in_ref[i].astype(jnp.float32)
        for part in range(parts):
            for half in range(2):
                at = half * hidden + part * LANES
                flat_ref[i, :, at : at + LANES] = spread[
                    i, pl.ds(part * 2 + half, width, stride=2 * parts), :
                ].astype(jnp.bfloat16)
        expert = (lax.axis_index("row") * steps + step) * each + i
        active, gate_up_grad, shares = expert_terms(
            dot(flat_ref[i], rows_ref[:, :width], 0, 1),
            dot(out_ref[i], grads_ref[...]),
            weights[pl.ds(expert, 1), :],
        )
        share[pl.ds(expert, 1), :] = jnp.sum(shares, axis=0, keepdims=True)
        moe_acc[...] += dot(active, out_ref[i], 0, 0)
        back_acc[...] += dot(gate_up_grad, flat_ref[i], 0, 1)
        in_sum[i] = dot(gate_up_grad, rows_ref[:, :width]).astype(jnp.bfloat16)
        out_sum[i] = dot(active, grads_ref[...], 1, 1).astype(jnp.bfloat16)

    @pl.when(step == steps - 1)
    def _():
        moe_ref[...] = moe_acc[...].astype(jnp.bfloat16)
        back_ref[:, :width] = back_acc[...].astype(jnp.bfloat16)
        back_ref[:, width:] = share[...].T.astype(jnp.bfloat16)
        moves.relay([1])
        moves.finish()


def local_experts(sizes, number, rows, grads, w_in, w_out, sent_grads, sent_rows):
    tokens, wide = rows.shape
    experts, hidden, width = w_out.shape
    each = 1
    low = jnp.bfloat16
    kinds, shapes, sems = planned(
        sizes,
        [
            ("gather", sent_grads, True, sent_grads.shape[0]),
            ("gather", sent_rows, True, sent_rows.shape[0]),
        ],
    )
    whole = lambda s: pl.BlockSpec(s, lambda e: (0,) * len(s))
    some = lambda s: pl.BlockSpec((each,) + s[1:], lambda e: (e,) + (0,) * (len(s) - 1))
    outs = [
        (tokens, width),
        (tokens, wide),
        (experts, width, 2 * hidden),
        (experts, 2 * hidden, width),
        (experts, hidden, width),
    ]
    return pl.pallas_call(
        functools.partial(local_experts_body, sizes, kinds),
        grid=(experts // each,),
        in_specs=[
            whole(rows.shape),
            whole(grads.shape),
            some(w_in.shape),
            some(w_out.shape),
            HBM,
            HBM,
        ],
        out_specs=(whole(outs[0]), whole(outs[1]), *[some(s) for s in outs[2:]], HBM, HBM),
        out_shape=tuple(jax.ShapeDtypeStruct(s, low) for s in outs) + tuple(shapes),
        scratch_shapes=[
            pltpu.VMEM((tokens, width), jnp.float32),
            pltpu.VMEM((tokens, width), jnp.float32),
            pltpu.VMEM((LANES, tokens), jnp.float32),
            pltpu.VMEM((LANES // 2, tokens), jnp.float32),
            pltpu.VMEM((each,) + w_in.shape[1:], jnp.float32),
        ]
        + sems,
        compiler_params=pltpu.CompilerParams(collective_id=number, has_side_effects=True),
        name="local_experts",
    )(rows, grads, w_in, w_out, sent_grads, sent_rows)


def cover_body(sizes, kinds, experts, first, in_ref, out_ref, in_part, out_part, rows_far, grads_first, grads_second, grads_rest, *refs):
    count = len(kinds)
    sources, in_sum, out_sum = refs[:count], refs[count], refs[count + 1]
    targets = refs[count + 2 : 2 * count + 2]
    rows, grads, weights, whole, turned, load_sem, *rest = refs[2 * count + 2 :]
    sums, sems = rest[:-3], rest[-3:]
    step = pl.program_id(0)
    layers, width, tokens = grads.shape
    hidden = out_ref.shape[1]
    moves = Moves(sizes, kinds, sources, targets, sems)

    @pl.when(step == 0)
    def _():
        loads = [
            pltpu.make_async_copy(rows_far, rows, load_sem.at[0]),
            pltpu.make_async_copy(grads_first, grads.at[pl.ds(0, 1)], load_sem.at[1]),
            pltpu.make_async_copy(grads_second, grads.at[pl.ds(1, 1)], load_sem.at[2]),
            pltpu.make_async_copy(grads_rest, grads.at[pl.ds(2, layers - 2)], load_sem.at[3]),
        ]
        for load in loads:
            load.start()
        moves.barrier()
        moves.start()
        for load in loads:
            load.wait()
        for i in range(layers):
            weights[i] = weight_rows(rows[i * tokens : (i + 1) * tokens, width:])

    index = lax.axis_index("row") * experts + first + step

    def part_of(at, pieces):
        block = rows[pl.ds(pl.multiple_of(at * tokens, tokens), pieces * tokens), :width]
        weight = jnp.concatenate(
            [weights[at + i, pl.ds(index, 1), :] for i in range(pieces)], axis=1
        )
        active_grad = jnp.concatenate(
            [dot(out_ref[0], grads[at + i]) for i in range(pieces)], axis=1
        )
        active, gate_up_grad, _ = expert_terms(dot(in_ref[0], block, 0, 1), active_grad, weight)
        out_total = functools.reduce(
            jnp.add,
            [
                dot(active[:, i * tokens : (i + 1) * tokens], grads[at + i], 1, 1)
                for i in range(pieces)
            ],
        )
        return dot(gate_up_grad, block), out_total

    if not sums:
        in_total, out_total = part_of(0, layers)
    else:
        in_acc, out_acc = sums
        in_acc[...] = jnp.zeros_like(in_acc)
        out_acc[...] = jnp.zeros_like(out_acc)

        def more(i, carry):
            in_more, out_more = part_of(i, 1)
            in_acc[...] += in_more
            out_acc[...] += out_more
            return carry

        lax.fori_loop(0, layers, more, 0)
        in_total, out_total = in_acc[...], out_acc[...]
    whole[...] = in_total
    parts = hidden // LANES

    def turn(i, carry):
        at = pl.ds(pl.multiple_of(i * LANES, LANES), LANES)
        first = lax.rem(i, parts) * 2 + i // parts
        rows_of = pl.ds(first, width, stride=2 * parts)
        turned[rows_of, :] = (whole[at, :] + in_part[0, at, :].astype(jnp.float32)).T
        return carry

    lax.fori_loop(0, 2 * parts, turn, 0)

    def narrow(i, carry):
        at = pl.ds(pl.multiple_of(i * width, width), width)
        in_sum[0, at, :] = turned[at, :].astype(jnp.bfloat16)
        return carry

    lax.fori_loop(0, 2 * parts, narrow, 0)
    out_sum[0] = (out_total + out_part[0].astype(jnp.float32)).astype(jnp.bfloat16)

    @pl.when(step == pl.num_programs(0) - 1)
    def _():
        moves.relay()
        moves.finish()


def cover(sizes, name, number, first, count, work, *items):
    w_in, w_out, in_part, out_part, rows_far, *grads_far = work
    layers = sum(g.shape[0] for g in grads_far)
    width, tokens = grads_far[0].shape[1:]
    experts, hidden, _ = w_out.shape
    kinds, shapes, sems = planned(sizes, items)
    each = lambda s: pl.BlockSpec((1,) + s[1:], lambda e: (first + e, 0, 0))
    out = lambda s: pl.BlockSpec((1,) + s[1:], lambda e: (e, 0, 0))
    turned = (width * 2 * hidden // LANES, LANES)
    outs = [(count,) + turned, (count, hidden, width)]
    sums = [(2 * hidden, width), (hidden, width)] if layers > 4 else []
    return pl.pallas_call(
        functools.partial(cover_body, sizes, kinds, experts, first),
        grid=(count,),
        in_specs=[each(a.shape) for a in work[:4]] + [HBM] * (len(work) - 4 + len(items)),
        out_specs=tuple(out(s) for s in outs) + (HBM,) * len(items),
        out_shape=tuple(jax.ShapeDtypeStruct(s, jnp.bfloat16) for s in outs) + tuple(shapes),
        scratch_shapes=[
            pltpu.VMEM(rows_far.shape, jnp.bfloat16),
            pltpu.VMEM((layers, width, tokens), jnp.bfloat16),
            pltpu.VMEM((layers, LANES // 2, tokens), jnp.float32),
            pltpu.VMEM((2 * hidden, width), jnp.float32),
            pltpu.VMEM(turned, jnp.float32),
            pltpu.SemaphoreType.DMA((1 + len(grads_far),)),
        ]
        + [pltpu.VMEM(s, jnp.float32) for s in sums]
        + sems,
        compiler_params=pltpu.CompilerParams(collective_id=number, has_side_effects=True),
        name=name,
    )(*work, *[item[1] for item in items])


def outputs_body(counts, *refs):
    pieces = len(counts)
    in_sums, out_sums = refs[:pieces], refs[pieces : 2 * pieces]
    blocks, in_blocks, gains, sums, output_all = refs[2 * pieces : 2 * pieces + 5]
    gin, gout, block_out, in_grad, gain_attn, gain_moe, query, pair, output, router = refs[
        2 * pieces + 5 :
    ]
    step = pl.program_id(0)
    width = gout.shape[2]

    @pl.when(step == 0)
    def _():
        for i in range(blocks.shape[0]):
            at = pl.ds(i * blocks.shape[1], blocks.shape[1])
            block_out[at, :] = blocks[i]
            in_grad[at, :] = in_blocks[i]
        gain_sum = jnp.sum(gains[...], axis=0)
        gain_attn[...] = gain_sum[0:1, :]
        gain_moe[...] = gain_sum[1:2, :]
        query[...] = sums[:width, :].astype(jnp.float32)
        pair[...] = sums[width : 2 * width, :].astype(jnp.float32)
        for i in range(width // LANES):
            at = slice(i * LANES, (i + 1) * LANES)
            output[:, at] = output_all[at, :].astype(jnp.float32)
        router[...] = sums[2 * width : 2 * width + router.shape[0], :].astype(jnp.float32)

    first = 0
    for count, in_sum, out_sum in zip(counts, in_sums, out_sums):

        @pl.when((step >= first) & (step < first + count))
        def _(in_sum=in_sum, out_sum=out_sum):
            gout[0] = out_sum[0].astype(jnp.float32)
            gin[0] = in_sum[0].astype(jnp.float32)

        first += count


def outputs(in_sums, out_sums, hidden, blocks, in_blocks, gains, sums, output_all, experts):
    counts = [s.shape[0] for s in in_sums]
    width = out_sums[0].shape[2]
    parts = hidden // LANES
    group, own, lanes = blocks.shape
    tokens = group * own
    once = lambda s: pl.BlockSpec(s, lambda e: (0,) * len(s))
    each = lambda s: pl.BlockSpec((1,) + s[1:], lambda e: (e, 0, 0))
    specs = []
    for arrays in (in_sums, out_sums):
        first = 0
        for array in arrays:
            count = array.shape[0]
            specs.append(
                pl.BlockSpec(
                    (1,) + array.shape[1:],
                    lambda e, first=first, count=count: (jnp.clip(e - first, 0, count - 1), 0, 0),
                )
            )
            first += count
    total = sum(counts)
    full = jnp.float32
    shapes = [
        ((total, width * 2 * parts, LANES), full),
        ((total, hidden, width), full),
        ((tokens, lanes), jnp.bfloat16),
        ((tokens, lanes), jnp.bfloat16),
        ((1, LANES), full),
        ((1, LANES), full),
        ((width, LANES), full),
        ((width, LANES), full),
        ((LANES, width), full),
        ((experts, LANES), full),
    ]
    gin, *others = pl.pallas_call(
        functools.partial(outputs_body, counts),
        grid=(total,),
        in_specs=specs + [once(a.shape) for a in (blocks, in_blocks, gains, sums, output_all)],
        out_specs=(each(shapes[0][0]), each(shapes[1][0])) + tuple(once(s) for s, _ in shapes[2:]),
        out_shape=tuple(jax.ShapeDtypeStruct(*shape) for shape in shapes),
        name="outputs",
    )(*in_sums, *out_sums, blocks, in_blocks, gains, sums, output_all)
    gin = gin.reshape(total, width, parts, 2, LANES).transpose(0, 1, 3, 2, 4)
    return gin.reshape(total, width, 2, hidden), *others


def local(
    sizes,
    tokens,
    out_grad,
    doc_ids,
    expert_ids,
    gain_attn,
    w_query,
    w_key_value,
    w_output,
    gain_moe,
    w_router,
    w_expert_in,
    w_expert_out,
):
    rows, cols, depth = sizes
    group = rows * cols
    tok_rows, feat_local = tokens.shape
    width = w_query.shape[0]
    experts = w_router.shape[1]
    expert_local, hidden = w_expert_out.shape[0], w_expert_out.shape[1]
    longest_doc = min(LONGEST, tok_rows * depth // 2)
    hop_count = longest_doc // tok_rows
    own = tok_rows // group
    low, full = jnp.bfloat16, jnp.float32
    layer = lax.axis_index("dp")
    me = lax.axis_index("row") * cols + lax.axis_index("col")
    everyone = list(range(1, depth))
    hops = list(range(1, hop_count + 1))

    tokens_blocks, gains, router, docs_far, grads_shifted, grad_blocks = exchange(
        sizes,
        "gather_tokens",
        0,
        ("gather", tokens, False, 2),
        ("gather", jnp.stack([gain_attn, gain_moe])),
        ("gather", w_router.T),
        ("shift", doc_ids.reshape(-1, LANES), everyone, False),
        ("shift", out_grad, everyone, False),
        ("gather", out_grad, False, 2),
    )

    lanes = jnp.arange(LANES, dtype=jnp.int32)
    frequencies = ROPE_BASE ** ((lanes % TURN).astype(full) * (-1.0 / TURN))
    positions = (layer * tok_rows + jnp.arange(tok_rows, dtype=jnp.int32)).astype(full)
    angles = positions[:, None] * frequencies[None, :]
    cosine = jnp.cos(angles)
    sine = jnp.sin(angles) * jnp.where(lanes % (2 * TURN) < TURN, -1.0, 1.0)[None, :]

    w_pair = w_key_value.reshape(width, -1)
    block = (tok_rows, LANES)
    turned = (LANES, tok_rows)
    normed, query, pair, tokens_own, grad_own, grads_near, far_turned = call(
        project_body,
        "project",
        [
            ((tok_rows, width), low),
            (block, low),
            (block, low),
            ((own, width), low),
            ((own, width), low),
            ((group,) + turned, low),
            ((depth - 1,) + turned, low),
        ],
        tokens_blocks,
        gains,
        w_query,
        w_pair,
        cosine,
        sine,
        grad_blocks,
        grads_shifted,
    )
    far, output_blocks = exchange(
        sizes, "shift_pairs", 1, ("shift", pair, hops, False), ("gather", w_output, False, 4)
    )
    output_full = output_blocks.reshape(-1, width)

    stack = (hop_count + 1,) + block
    twice = (2 * tok_rows, LANES)
    mixed, log_total, start, grads_first = hosted(
        attend_body,
        "attend",
        [(block, low), ((2 * tok_rows, 1), full), ((tok_rows, 1), jnp.int32)],
        query,
        pair,
        far,
        doc_ids.reshape(-1, LANES),
        docs_far,
        scratch=[
            pltpu.VMEM(stack, low),
            pltpu.VMEM(stack, low),
            pltpu.VMEM(twice, low),
            pltpu.VMEM(twice, full),
        ],
        sizes=sizes,
        number=10,
        items=[("gather", far_turned[:1], True)],
    )
    (mixed_own,) = exchange(
        sizes, "swap_mixed", 2, ("swap", mixed.reshape(group, own, LANES))
    )
    rows_own, middle, weights = call(
        middle_body,
        "middle",
        [((own, width + LANES), low), ((own, width), full), ((own, LANES), full)],
        mixed_own,
        tokens_own,
        output_full,
        gains,
        router,
        expert_ids.T,
        scratch=[pltpu.VMEM(expert_ids.shape, full)],
    )
    rows_blocks, rows_shifted, grads_second = exchange(
        sizes,
        "gather_rows",
        3,
        ("gather", rows_own, False, 2),
        ("shift", rows_own, everyone, False),
        ("gather", far_turned[1:2], True),
    )
    rows_near = rows_blocks.reshape(tok_rows, -1)
    parts = hidden // LANES
    in_rows = w_expert_in.reshape(expert_local, width, 2, parts, LANES)
    in_rows = in_rows.transpose(0, 1, 3, 2, 4).reshape(expert_local, -1, LANES)
    moe_partial, back_partial, in_flat, in_part, out_part, grads_far, rows_far = local_experts(
        sizes,
        9,
        rows_near,
        grads_near.reshape(width, tok_rows),
        in_rows,
        w_expert_out,
        far_turned[2:],
        rows_shifted,
    )
    rows_far = rows_far.reshape((depth - 1) * tok_rows, -1)
    grads_far = [
        g.reshape(-1, width, tok_rows) for g in (grads_first, grads_second, grads_far)
    ]
    work = (in_flat, w_expert_out, in_part, out_part, rows_far, *grads_far)
    share = expert_local // 4
    unit = 16 * depth
    in_sums, out_sums = [], []

    def beneath(name, number, *items):
        in_sum, out_sum, *moved = cover(
            sizes, name, number, len(in_sums) * share, share, work, *items
        )
        in_sums.append(in_sum)
        out_sums.append(out_sum)
        return moved

    (back_blocks,) = beneath("swap_back", 4, ("swap", back_partial.reshape(group, own, -1)))
    middle_grad, attn_grad, logit_grad, gain_moe_part = call(
        middle_back_body,
        "middle_back",
        [
            ((own, width), full),
            ((own, width), low),
            ((own, LANES), low),
            ((1, width), full),
        ],
        back_blocks,
        grad_own,
        middle,
        weights,
        gains,
        router,
    )
    attn_grad_blocks, logit_blocks = exchange(
        sizes,
        "gather_attn_grad",
        5,
        ("gather", attn_grad, False, 2),
        ("gather", logit_grad),
    )
    query_grad, pair_grad, far_grad, output_sum = call(
        attend_back_body,
        "attend_back",
        [(block, low), (block, full), ((hop_count,) + block, low), ((group, LANES, LANES), low)],
        attn_grad_blocks.reshape(tok_rows, width),
        w_output,
        query,
        pair,
        far,
        start,
        log_total,
        mixed,
        cosine,
        sine,
        scratch=[
            pltpu.VMEM(stack, low),
            pltpu.VMEM(stack, low),
            pltpu.VMEM(twice, low),
            pltpu.VMEM(twice, low),
            pltpu.VMEM(twice, full),
            pltpu.VMEM(stack, full),
            pltpu.VMEM(stack, full),
        ],
    )
    returned, moe_blocks, output_turned = beneath(
        "shift_grads",
        6,
        ("shift", far_grad, [-d for d in hops], True),
        ("swap", moe_partial.reshape(group, own, width)),
        ("turn", output_sum.reshape(depth, width // depth, LANES)),
    )
    length = (2 * width + LANES + unit - 1) // unit * unit
    partial, sums, output_summed, gain_parts = call(
        project_back_body,
        "project_back",
        [
            ((tok_rows, width), low),
            ((length, LANES), low),
            ((width // depth, LANES), low),
            ((group, 8, LANES), full),
        ],
        query_grad,
        pair_grad,
        returned,
        normed,
        w_query,
        w_pair,
        cosine,
        sine,
        output_turned,
        logit_blocks.reshape(tok_rows, LANES),
        rows_near,
        gains,
        gain_moe_part,
    )
    partial_blocks, sums_turned, output_all, gain_blocks = beneath(
        "swap_partial",
        7,
        ("swap", partial.reshape(group, own, width)),
        ("turn", sums.reshape(depth, length // depth, LANES)),
        ("collect", output_summed),
        ("swap", gain_parts),
    )
    pieces = (group, own, LANES)
    block_out, in_grad, gain_sum, summed = call(
        results_body,
        "results",
        [
            (pieces, low),
            (pieces, low),
            ((8, LANES), full),
            ((length // depth, LANES), low),
        ],
        partial_blocks,
        moe_blocks,
        tokens_own,
        middle,
        middle_grad,
        gains,
        gain_blocks,
        sums_turned,
    )
    block_out, in_grad, gain_all, sums = beneath(
        "swap_results",
        8,
        ("swap", block_out),
        ("swap", in_grad),
        ("collect", gain_sum),
        ("collect", summed),
    )
    grad_in, grad_out, block_out, in_grad, gain_attn_sum, gain_moe_sum, query_sum, pair_sum, output_sum, router_sum = outputs(
        in_sums,
        out_sums,
        hidden,
        block_out,
        in_grad,
        gain_all,
        sums.reshape(length, LANES),
        output_all.reshape(width, LANES),
        experts,
    )
    return (
        block_out,
        in_grad,
        gain_attn_sum.reshape(LANES),
        query_sum,
        pair_sum.reshape(w_key_value.shape),
        output_sum,
        gain_moe_sum.reshape(LANES),
        router_sum.T,
        grad_in,
        grad_out,
    )


def solution(mesh):
    in_specs = (
        P("dp", ("row", "col")),
        P("dp", ("row", "col")),
        P("dp"),
        P("dp", None),
        P(("row", "col")),
        P(None, ("row", "col")),
        P(None, ("row", "col"), None),
        P(("row", "col"), None),
        P(("row", "col")),
        P(("row", "col"), None),
        P("row", None, None, "col"),
        P("row", "col", None),
    )
    out_specs = (
        P("dp", ("row", "col")),
        P("dp", ("row", "col")),
        P(("row", "col")),
        P(None, ("row", "col")),
        P(None, ("row", "col"), None),
        P(("row", "col"), None),
        P(("row", "col")),
        P(("row", "col"), None),
        P("row", None, None, "col"),
        P("row", "col", None),
    )
    sizes = (mesh.shape["row"], mesh.shape["col"], mesh.shape["dp"])
    return jax.shard_map(
        functools.partial(local, sizes),
        mesh=mesh,
        in_specs=in_specs,
        out_specs=out_specs,
        check_vma=False,
    )
```

profile of v0, /device:TPU:0, one launch (start us, length us, event | category | flops | bytes accessed | tf_op | source)
XLA Modules:
  0.0 258.6 jit_solution(8687254360561760923)
XLA Ops:
  0.6 1.2 pad_maximum_fusion.refs_1_
  1.9 1.8 fusion
  3.7 21.5 %gather_tokens.1 = (bf16[8,512,128]{2,1,0:T(8,128)(2,1)}, bf16[8,2,128]{2,1,0:T(2,128)(2,1)}, bf16[8,32,128]{2,1,0:T(8,128)(2,1)}, s32[3,4,128]{2,1,0:T(4,128)},...) custom-call(bf16[512,128]{1,0:T(8,128)(2,1)} %refs_0_.1, bf16[2,128]{1,0:T(2,128)(2,1)} %pad_maximum_fusion.refs_1_, ...), custom_call_target="tpu_custom_call" | custom-call | tf_op jit(solution)/shard_map/gather_tokens/pallas_call | solution.py:205
  25.2 4.4 %project.1 = (bf16[512,1024]{1,0:T(8,128)(2,1)}, bf16[512,128]{1,0:T(8,128)(2,1)}, bf16[512,128]{1,0:T(8,128)(2,1)}, bf16[64,1024]{1,0:T(8,128)(2,1)}, bf16[64,1...) custom-call(bf16[8,512,128]{2,1,0:T(8,128)(2,1)} %get-tuple-element.90.blocks, ...), custom_call_target="tpu_custom_call" | custom-call | tf_op jit(solution)/shard_map/project/pallas_call | solution.py:227
  29.6 1.8 fusion.4
  31.4 17.1 %shift_pairs.1 = (bf16[2,512,128]{2,1,0:T(8,128)(2,1)}, bf16[8,128,1024]{2,1,0:T(8,128)(2,1)}) custom-call(bf16[512,128]{1,0:T(8,128)(2,1)} %get-tuple-element.95.refs_0_.refs_1_.pair, bf16[128,1024]{1,0:T(8,128)(2,1)} %w_output.1), custom_call_target="tpu_custom_call" | custom-call | tf_op jit(solution)/shard_map/shift_pairs/pallas_call | solution.py:205
  48.5 13.3 %attend.1 = (bf16[512,128]{1,0:T(8,128)(2,1)}, f32[1024,1]{1,0:T(8,128)}, s32[512,1]{1,0:T(8,128)}, bf16[1,8,128,512]{3,2,1,0:T(8,128)(2,1)}) custom-call(bf16[512,128]{1,0:T(8,128)(2,1)} %get-tuple-element.94.refs_0_.query, bf16[512,128]{1,0:T(8,128)(2,1)} %get-tuple-element.95.refs_0_.refs_1_.pair, bf16[2,512,128]{2,1,0:T(8,128)(2,1)} %get-tuple-element.96.refs_2_.far, ...), custom_call_target="tpu_custom_call" | custom-call | tf_op jit(solution)/shard_map/attend/pallas_call | solution.py:253
  61.9 5.3 %swap_mixed.1.mixed = bf16[8,64,128]{2,1,0:T(8,128)(2,1)} custom-call(bf16[8,64,128]{2,1,0:T(8,128)(2,1)} %bitcast.68), custom_call_target="tpu_custom_call" | custom-call | tf_op jit(solution)/shard_map/swap_mixed/pallas_call | solution.py:205
  67.2 3.9 %middle.1 = (bf16[64,1152]{1,0:T(8,128)(2,1)}, f32[64,1024]{1,0:T(8,128)}, f32[64,128]{1,0:T(8,128)}) custom-call(bf16[8,64,128]{2,1,0:T(8,128)(2,1)} %swap_mixed.1.mixed, bf16[64,1024]{1,0:T(8,128)(2,1)} %get-tuple-element.100.own, bf16[1024,1024]{1,0:T(8,128)(2,1)} %bitcast.58, bf16[8,2,128]{2,1,0:T(2,128)(2,1)} %get-tuple-element.91.gains, ...), custom_call_target="tpu_custom_call" | custom-call | tf_op jit(solution)/shard_map/middle/pallas_call | solution.py:227
  71.1 18.5 %gather_rows.1 = (bf16[8,64,1152]{2,1,0:T(8,128)(2,1)}, bf16[3,64,1152]{2,1,0:T(8,128)(2,1)}, bf16[1,8,128,512]{3,2,1,0:T(8,128)(2,1)}) custom-call(bf16[64,1152]{1,0:T(8,128)(2,1)} %get-tuple-element.103.refs_0_.refs_1_, bf16[64,1152]{1,0:T(8,128)(2,1)} %get-tuple-element.103.refs_0_.refs_1_, bf16[1,128,512]{2,1,0:T(8,128)(2,1)} %get-tuple-element.181.refs_2_), custom_call_target="tpu_custom_call" | custom-call | tf_op jit(solution)/shard_map/gather_rows/pallas_call | solution.py:205
  89.6 35.2 %local_experts.1 = (bf16[512,1024]{1,0:T(8,128)(2,1)}, bf16[512,1152]{1,0:T(8,128)(2,1)}, bf16[8,1024,512]{2,1,0:T(8,128)(2,1)}, bf16[8,512,1024]{2,1,0:T(8,128)...) custom-call(bf16[512,1152]{1,0:T(8,128)(2,1)} %bitcast.56, ...), custom_call_target="tpu_custom_call" | custom-call | tf_op jit(solution)/shard_map/local_experts/pallas_call | solution.py:645
  124.9 19.6 %swap_back.1 = (bf16[2,4096,128]{2,1,0:T(8,128)(2,1)}, bf16[2,256,1024]{2,1,0:T(8,128)(2,1)}, bf16[8,64,1152]{2,1,0:T(8,128)(2,1)}) custom-call(bf16[8,1024,512]{2,1,0:T(8,128)(2,1)} %get-tuple-element.107.in_ref, bf16[8,256,1024]{2,1,0:T(8,128)(2,1)} %out_ref.9, bf16[8,512,1024]{2,1,0:T(8,128)(2,1)} %get-tuple-element.108.in_part, ...), custom_call_target="tpu_custom_call" | custom-call | tf_op jit(solution)/shard_map/swap_back/pallas_call | solution.py:771
  144.5 2.7 %middle_back.1 = (f32[64,1024]{1,0:T(8,128)}, bf16[64,1024]{1,0:T(8,128)(2,1)}, bf16[64,128]{1,0:T(8,128)(2,1)}, f32[1,1024]{1,0:T(1,128)}) custom-call(bf16[8,64,1152]{2,1,0:T(8,128)(2,1)} %get-tuple-element.116.back, bf16[64,1024]{1,0:T(8,128)(2,1)} %get-tuple-element.117.out_grad, f32[64,1024]{1,0:T(8,128)} %get-tuple-element.118.middle, ...), custom_call_target="tpu_custom_call" | custom-call | tf_op jit(solution)/shard_map/middle_back/pallas_call | solution.py:227
  147.2 12.0 %gather_attn_grad.1 = (bf16[8,64,1024]{2,1,0:T(8,128)(2,1)}, bf16[8,64,128]{2,1,0:T(8,128)(2,1)}) custom-call(bf16[64,1024]{1,0:T(8,128)(2,1)} %get-tuple-element.120.refs_0_, bf16[64,128]{1,0:T(8,128)(2,1)} %get-tuple-element.121.refs_1_), custom_call_target="tpu_custom_call" | custom-call | tf_op jit(solution)/shard_map/gather_attn_grad/pallas_call | solution.py:205
  159.2 10.2 %attend_back.1 = (bf16[512,128]{1,0:T(8,128)(2,1)}, f32[512,128]{1,0:T(8,128)}, bf16[2,512,128]{2,1,0:T(8,128)(2,1)}, bf16[8,128,128]{2,1,0:T(8,128)(2,1)}) custom-call(bf16[512,1024]{1,0:T(8,128)(2,1)} %bitcast.63, bf16[128,1024]{1,0:T(8,128)(2,1)} %w_output.1, bf16[512,128]{1,0:T(8,128)(2,1)} %get-tuple-element.94.refs_0_.query, ...), custom_call_target="tpu_custom_call" | custom-call | tf_op jit(solution)/shard_map/attend_back/pallas_call | solution.py:227
  169.4 20.9 %shift_grads.1 = (bf16[2,4096,128]{2,1,0:T(8,128)(2,1)}, bf16[2,256,1024]{2,1,0:T(8,128)(2,1)}, bf16[2,512,128]{2,1,0:T(8,128)(2,1)}, bf16[8,64,1024]{2,1,0:T(8,128)(2,1)}, bf16[4,256,128]{2,1,0:T(8,128)(2,1)}) custom-call(bf16[8,1024,512]{2,1,0:T(8,128)(2,1)} %get-tuple-element.107.in_ref, bf16[8,256,1024]{2,1,0:T(8,128)(2,1)} %out_ref.9, ...), custom_call_target="tpu_custom_call" | custom-call | tf_op jit(solution)/shard_map/shift_grads/pallas_call | solution.py:771
  190.3 4.5 %project_back.1 = (bf16[512,1024]{1,0:T(8,128)(2,1)}, bf16[2176,128]{1,0:T(8,128)(2,1)}, bf16[256,128]{1,0:T(8,128)(2,1)}, f32[8,8,128]{2,1,0:T(8,128)}) custom-call(bf16[512,128]{1,0:T(8,128)(2,1)} %get-tuple-element.129.query_grad, f32[512,128]{1,0:T(8,128)} %get-tuple-element.130.pair_grad, bf16[2,512,128]{2,1,0:T(8,128)(2,1)} %get-tuple-element.131.returned, ...), custom_call_target="tpu_custom_call" | custom-call | tf_op jit(solution)/shard_map/project_back/pallas_call | solution.py:227
  194.8 24.1 %swap_partial.1 = (bf16[2,4096,128]{2,1,0:T(8,128)(2,1)}, bf16[2,256,1024]{2,1,0:T(8,128)(2,1)}, bf16[8,64,1024]{2,1,0:T(8,128)(2,1)}, bf16[4,544,128]{2,1,0:T(8...) custom-call(bf16[8,1024,512]{2,1,0:T(8,128)(2,1)} %get-tuple-element.107.in_ref, ...), custom_call_target="tpu_custom_call" | custom-call | tf_op jit(solution)/shard_map/swap_partial/pallas_call | solution.py:771
  219.0 3.1 %results.1 = (bf16[8,64,128]{2,1,0:T(8,128)(2,1)}, bf16[8,64,128]{2,1,0:T(8,128)(2,1)}, f32[8,128]{1,0:T(8,128)}, bf16[544,128]{1,0:T(8,128)(2,1)}) custom-call(bf16[8,64,1024]{2,1,0:T(8,128)(2,1)} %get-tuple-element.141.blocks, bf16[8,64,1024]{2,1,0:T(8,128)(2,1)} %get-tuple-element.142.moe, bf16[64,1024]{1,0:T(8,128)(2,1)} %get-tuple-element.100.own, ...), custom_call_target="tpu_custom_call" | custom-call | tf_op jit(solution)/shard_map/results/pallas_call | solution.py:227
  222.1 20.6 %swap_results.1 = (bf16[2,4096,128]{2,1,0:T(8,128)(2,1)}, bf16[2,256,1024]{2,1,0:T(8,128)(2,1)}, bf16[8,64,128]{2,1,0:T(8,128)(2,1)}, bf16[8,64,128]{2,1,0:T(8,1...) custom-call(bf16[8,1024,512]{2,1,0:T(8,128)(2,1)} %get-tuple-element.107.in_ref, ...), custom_call_target="tpu_custom_call" | custom-call | tf_op jit(solution)/shard_map/swap_results/pallas_call | solution.py:771
  242.7 15.8 %outputs.1 = (f32[8,4096,128]{2,1,0:T(8,128)}, f32[8,256,1024]{2,1,0:T(8,128)}, bf16[512,128]{1,0:T(8,128)(2,1)}, bf16[512,128]{1,0:T(8,128)(2,1)}, f32[1,128]{1...) custom-call(bf16[2,4096,128]{2,1,0:T(8,128)(2,1)} %get-tuple-element, ...), custom_call_target="tpu_custom_call" | custom-call | tf_op jit(solution)/shard_map/outputs/pallas_call | solution.py:863
  (2 shorter events, 0.0 us)
where the time goes:
time: 259 us
  Pallas kernels  253 us (98%)
  other arithmetic  3.03 us (1%)
    pallas_call x4, Pallas kernels, cover(): pl.pallas_call(functools.partial(cover_body, sizes, kinds, experts, first...  85.2 us
    pallas_call x5, Pallas kernels, exchange(): pl.pallas_call(functools.partial(exchange_body, sizes, kinds), out_shape=...  74.5 us
    pallas_call x1, Pallas kernels, local_experts(): pl.pallas_call(functools.partial(local_experts_body, sizes, kinds), grid=...  35.2 us
    pallas_call x6, Pallas kernels, call(): pl.pallas_call(body, out_shape=tuple((jax.ShapeDtypeStruct(*shape) for sh...  28.8 us
    pallas_call x1, Pallas kernels, outputs(): pl.pallas_call(functools.partial(outputs_body, counts), grid=(total,), in...  15.8 us
    pallas_call x1, Pallas kernels, hosted(): pl.pallas_call(whole, out_shape=tuple((jax.ShapeDtypeStruct(*shape) for s...  13.3 us

commit v1 on v0

--- a/solution.py
+++ b/solution.py
@@ -37,6 +37,10 @@
         rows, cols, depth = self.sizes
         return {"row": index // cols, "col": lax.rem(index, cols)}
 
+    def across(self, row):
+        low = lax.rem(row, 2)
+        return row + 1 - 2 * low, lax.rem(row + 2, 4), lax.rem(row + 3 - 2 * low, 4)
+
     def barrier(self):
         rows, cols, depth = self.sizes
         row, col, layer, me = self.place()
@@ -44,12 +48,12 @@
         names = [kind[0] for kind in self.kinds]
         barrier = pltpu.get_barrier_semaphore()
         partners = []
-        if "swap" in names:
+        if "swap" in names or "share" in names:
             for k in range(1, group):
                 partners.append(self.member(lax.rem(me + k, group)))
         elif "gather" in names:
-            for k in range(1, rows):
-                partners.append({"row": lax.rem(row + k, rows)})
+            for other in self.across(row)[:2]:
+                partners.append({"row": other})
             for k in range(1, cols):
                 partners.append({"col": lax.rem(col + k, cols)})
         shifts = set()
@@ -57,30 +61,40 @@
             if kind[0] == "shift":
                 for d in kind[1]:
                     shifts |= {d % depth, -d % depth}
-            elif kind[0] in ("turn", "collect"):
+            elif kind[0] == "turn":
                 shifts |= set(range(1, depth))
         for k in sorted(shifts - {0}):
             partners.append({"dp": lax.rem(layer + k, depth)})
+        ends = [(layer > 0, layer - 1), (layer < depth - 1, layer + 1)]
+        ends = ends if "line" in names and not shifts else []
         for partner in partners:
             pl.semaphore_signal(barrier, inc=1, device_id=partner, device_id_type=MESH)
-        pl.semaphore_wait(barrier, len(partners))
-
-    def copies(self, only):
+        for there, other in ends:
+
+            @pl.when(there)
+            def _(device={"dp": other}):
+                pl.semaphore_signal(barrier, inc=1, device_id=device, device_id_type=MESH)
+
+        expected = len(partners)
+        for there, _ in ends:
+            expected = expected + there.astype(jnp.int32)
+        pl.semaphore_wait(barrier, expected)
+
+    def plan(self, only):
         rows, cols, depth = self.sizes
         row, col, layer, me = self.place()
         group = rows * cols
-        slot = 0
-        lists = []
-
-        def remote(source, target, device):
-            nonlocal slot
-            slot += 1
+        slots = iter(range(self.send_sem.shape[0]))
+        starts, relays, sends, arrivals, local = [], [], [], [], []
+
+        def remote(source, target, device, slot=None):
+            slot = next(slots) if slot is None else slot
             return functools.partial(
                 pltpu.make_async_remote_copy,
                 src_ref=source,
                 dst_ref=target,
-                send_sem=self.send_sem.at[slot - 1],
-                recv_sem=self.recv_sem.at[slot - 1],
+                send_sem=self.send_sem.at[slot],
+                recv_sem=self.recv_sem.at[slot],
                 device_id=device,
                 device_id_type=MESH,
             )
@@ -88,75 +102,147 @@
         for index, (kind, source, target) in enumerate(
             zip(self.kinds, self.sources, self.targets)
         ):
-            direct, relayed, local = [], [], []
+            item = [], [], [], [], []
+            begin, follow, sent, got, stay = item
 
             def keep(source, target):
                 sem = self.local_sem.at[index]
-                local.append(functools.partial(pltpu.make_async_copy, source, target, sem))
+                stay.append(functools.partial(pltpu.make_async_copy, source, target, sem))
+
+            def direct(source, target, device):
+                copy = None, remote(source, target, device)
+                begin.append(copy)
+                sent.append(copy)
+                got.append(copy)
 
             if kind[0] == "gather":
                 second, parts = kind[1:]
                 size = source.shape[0] // parts
-
-                def at(i, part):
-                    some = pl.ds(part * size, size)
-                    return target.at[some, i] if second else target.at[i, some]
+                beside, above, away = self.across(row)
+
+                def at(other, part, piece=None):
+                    member = other * cols + col
+                    first, length, deep = part * size, size, ()
+                    if piece is not None and size % 2 == 0:
+                        length = size // 2
+                        first = first + piece * length
+                    elif piece is not None:
+                        inner = source.shape[1] // 2
+                        deep = (pl.ds(piece * inner, inner),)
+                    some = pl.ds(first, length)
+                    return target.at[(some, member) + deep if second else (member, some) + deep]
+
+                def to_mates(piece):
+                    made = []
+                    for j in range(1, cols):
+                        copy = None, remote(piece, piece, {"col": lax.rem(col + j, cols)})
+                        made.append(copy)
+                        sent.append(copy)
+                        got.append(copy)
+                    return made
 
                 for part in range(parts):
                     some = source.at[pl.ds(part * size, size)]
-                    for k in range(1, rows):
-                        device = {"row": lax.rem(row + k, rows)}
-                        copy = remote(some, at(me, part), device)
-                        piece = at(lax.rem(row + rows - k, rows) * cols + col, part)
-                        nexts = [
-                            remote(piece, piece, {"col": lax.rem(col + j, cols)})
-                            for j in range(1, cols)
-                        ]
-                        relayed.append((copy, nexts))
-                    for k in range(1, cols):
-                        device = {"col": lax.rem(col + k, cols)}
-                        direct.append(remote(some, at(me, part), device))
+                    ways = []
+                    for near, other, piece in ((beside, above, 0), (above, beside, 1)):
+                        first = None, remote(some, at(row, part), {"row": near})
+                        passed = at(near, part, piece)
+                        onward = None, remote(passed, passed, {"row": other})
+                        begin.append(first)
+                        sent.extend([first, onward])
+                        ways.append((near, piece, first, onward))
+                    for near, piece, first, onward in ways:
+                        nexts = [onward] + to_mates(at(near, part))
+                        follow.append((2 + 3 * part, None, first[1], nexts))
+                    for near, piece, first, onward in ways:
+                        nexts = to_mates(at(away, part, piece))
+                        follow.append((2 + 3 * parts + part, None, onward[1], nexts))
+                    for j in range(1, cols):
+                        direct(some, at(row, part), {"col": lax.rem(col + j, cols)})
                 keep(source, target.at[:, me] if second else target.at[me])
-            elif kind[0] == "swap":
+            elif kind[0] in ("swap", "share"):
                 for k in range(1, group):
                     other = lax.rem(me + k, group)
-                    direct.append(remote(source.at[other], target.at[me], self.member(other)))
-                keep(source.at[me], target.at[me])
-            elif kind[0] in ("turn", "collect"):
+                    piece = source.at[other] if kind[0] == "swap" else source
+                    direct(piece, target.at[me], self.member(other))
+                keep(source.at[me] if kind[0] == "swap" else source, target.at[me])
+            elif kind[0] == "turn":
                 for k in range(1, depth):
                     other = lax.rem(layer + k, depth)
-                    piece = source.at[other] if kind[0] == "turn" else source
-                    direct.append(remote(piece, target.at[layer], {"dp": other}))
-                keep(source.at[layer] if kind[0] == "turn" else source, target.at[layer])
+                    direct(source.at[other], target.at[layer], {"dp": other})
+                keep(source.at[layer], target.at[layer])
+            elif kind[0] == "line":
+                absolute = kind[1]
+                for way in (1, -1):
+                    behind = layer if way == 1 else depth - 1 - layer
+                    onward = layer + way
+                    more = (onward >= 0) & (onward < depth)
+                    mine = [next(slots) for _ in range(1, depth)]
+
+                    def held(step, where, way=way):
+                        if step == 0:
+                            return source
+                        if absolute:
+                            return target.at[where - way * step]
+                        return target.at[step - 1 if way == 1 else depth - 1 - step]
+
+                    def sending(step, onward=onward, mine=mine, held=held):
+                        device = {"dp": onward}
+                        return remote(
+                            held(step - 1, layer), held(step, onward), device, mine[step - 1]
+                        )
+
+                    begin.append((more, sending(1)))
+                    for step in range(1, depth):
+                        sent.append((more & (behind >= step - 1), sending(step)))
+                        block = held(step, layer)
+                        arrival = remote(block, block, {"dp": onward}, mine[step - 1])
+                        nexts = [(more, sending(step + 1))] if step + 1 < depth else []
+                        follow.append((4 * step, behind >= step, arrival, nexts))
+                if absolute:
+                    keep(source, target.at[layer])
             else:
-                for at, d in enumerate(kind[1]):
-                    piece = source.at[at] if kind[2] else source
-                    device = {"dp": lax.rem(layer + d % depth, depth)}
-                    direct.append(remote(piece, target.at[at], device))
+                for at_slot, d in enumerate(kind[1]):
+                    piece = source.at[at_slot] if kind[2] else source
+                    direct(piece, target.at[at_slot], {"dp": lax.rem(layer + d % depth, depth)})
             if only is None or index in only:
-                lists.append((direct, relayed, local))
-        return tuple(sum((part[i] for part in lists), []) for i in range(3))
+                starts += begin
+                relays += follow
+                sends += sent
+                arrivals += got
+                local += stay
+        return starts, sorted(relays, key=lambda entry: entry[0]), sends, arrivals, local
+
+    def given(self, condition, action):
+        if condition is None:
+            action()
+        else:
+            pl.when(condition)(action)
 
     def start(self, only=None):
-        direct, relayed, local = self.copies(only)
-        for copy, _ in relayed:
+        starts, _, _, _, local = self.plan(only)
+        for condition, copy in starts:
+            self.given(condition, lambda copy=copy: copy().start())
+        for copy in local:
             copy().start()
-        for copy in direct + local:
-            copy().start()
 
     def relay(self, only=None):
-        for copy, nexts in self.copies(only)[1]:
-            copy().wait_recv()
-            for follower in nexts:
-                follower().start()
+        for _, condition, copy, nexts in self.plan(only)[1]:
+
+            def action(copy=copy, nexts=nexts):
+                copy().wait_recv()
+                for more, follower in nexts:
+                    self.given(more, lambda follower=follower: follower().start())
+
+            self.given(condition, action)
 
     def finish(self, only=None):
-        direct, relayed, local = self.copies(only)
-        for copy, nexts in relayed:
-            copy().wait_send()
-            for follower in nexts:
-                follower().wait()
-        for copy in direct + local:
+        _, _, sends, arrivals, local = self.plan(only)
+        for condition, copy in arrivals:
+            self.given(condition, lambda copy=copy: copy().wait_recv())
+        for condition, copy in sends:
+            self.given(condition, lambda copy=copy: copy().wait_send())
+        for copy in local:
             copy().wait()
 
 
@@ -168,20 +254,25 @@
         name, array = item[0], item[1]
         shape = array.shape
         if name == "gather":
+            assert rows == 4
             second, parts = (item[2:] + (False, 1)[len(item) - 2 :])[:2]
             kinds.append((name, second, parts))
             shape = (shape[0], group) + shape[1:] if second else (group,) + shape
-            copies += parts * ((rows - 1) * cols + cols - 1)
+            copies += parts * (4 + 5 * (cols - 1))
         elif name == "shift":
             distances, split = item[2], item[3]
             kinds.append((name, tuple(distances), split))
             shape = (len(distances),) + (shape[1:] if split else shape)
             copies += len(distances)
+        elif name == "line":
+            kinds.append((name, item[2]))
+            shape = (depth if item[2] else depth - 1,) + shape
+            copies += 2 * (depth - 1)
         else:
             kinds.append((name,))
-            if name == "collect":
-                shape = (depth,) + shape
-            copies += (group if name == "swap" else depth) - 1
+            if name == "share":
+                shape = (group,) + shape
+            copies += (depth if name == "turn" else group) - 1
         shapes.append(jax.ShapeDtypeStruct(shape, array.dtype))
     sems = [
         pltpu.SemaphoreType.DMA((copies,)),
@@ -232,33 +323,6 @@
         scratch_shapes=list(scratch),
         name=name,
     )(*arrays)
-
-
-def hosted(body, name, shapes, *arrays, scratch=(), sizes, number, items):
-    kinds, moved, sems = planned(sizes, items)
-    ins, count, outs = len(arrays), len(items), len(shapes)
-
-    def whole(*refs):
-        sources = refs[ins : ins + count]
-        made = refs[ins + count : ins + count + outs]
-        targets = refs[ins + count + outs : ins + 2 * count + outs]
-        rest = refs[ins + 2 * count + outs :]
-        moves = Moves(sizes, kinds, sources, targets, rest[len(scratch) :])
-        moves.barrier()
-        moves.start()
-        body(*refs[:ins], *made, *rest[: len(scratch)])
-        moves.relay()
-        moves.finish()
-
-    return pl.pallas_call(
-        whole,
-        out_shape=tuple(jax.ShapeDtypeStruct(*shape) for shape in shapes) + tuple(moved),
-        in_specs=[FULL] * ins + [HBM] * count,
-        out_specs=(FULL,) * outs + (HBM,) * count,
-        scratch_shapes=list(scratch) + sems,
-        compiler_params=pltpu.CompilerParams(collective_id=number, has_side_effects=True),
-        name=name,
-    )(*arrays, *[item[1] for item in items])
 
 
 def lanes_of(shape):
@@ -668,88 +732,119 @@
     )(rows, grads, w_in, w_out, sent_grads, sent_rows)
 
 
-def cover_body(sizes, kinds, experts, first, in_ref, out_ref, in_part, out_part, rows_far, grads_first, grads_second, grads_rest, *refs):
+class Sums:
+    def __init__(self, rows, grads, weights, whole, turned, load_sem, *sums):
+        self.rows, self.grads, self.weights = rows, grads, weights
+        self.whole, self.turned, self.load_sem, self.sums = whole, turned, load_sem, sums
+
+    def loads(self, rows_far, grads_far):
+        return [
+            pltpu.make_async_copy(rows_far, self.rows, self.load_sem.at[0]),
+            pltpu.make_async_copy(grads_far, self.grads, self.load_sem.at[1]),
+        ]
+
+    def ready(self):
+        layers, width, tokens = self.grads.shape
+        for i in range(layers):
+            self.weights[i] = weight_rows(self.rows[i * tokens : (i + 1) * tokens, width:])
+
+    def make(self, index, w_in, w_out, in_part, out_part):
+        layers, width, tokens = self.grads.shape
+        hidden = w_out.shape[0]
+
+        def part_of(at, pieces):
+            first = at * tokens if isinstance(at, int) else pl.multiple_of(at * tokens, tokens)
+            block = self.rows[pl.ds(first, pieces * tokens), :width]
+            weight = jnp.concatenate(
+                [self.weights[at + i, pl.ds(index, 1), :] for i in range(pieces)], axis=1
+            )
+            active_grad = jnp.concatenate(
+                [dot(w_out, self.grads[at + i]) for i in range(pieces)], axis=1
+            )
+            active, gate_up_grad, _ = expert_terms(dot(w_in, block, 0, 1), active_grad, weight)
+            out_total = functools.reduce(
+                jnp.add,
+                [
+                    dot(active[:, i * tokens : (i + 1) * tokens], self.grads[at + i], 1, 1)
+                    for i in range(pieces)
+                ],
+            )
+            return dot(gate_up_grad, block), out_total
+
+        if not self.sums:
+            self.whole[...], out_total = part_of(0, layers)
+        else:
+            self.whole[...] = jnp.zeros_like(self.whole)
+            (out_acc,) = self.sums
+            out_acc[...] = jnp.zeros_like(out_acc)
+
+            def more(i, carry):
+                in_more, out_more = part_of(i, 1)
+                self.whole[...] += in_more
+                out_acc[...] += out_more
+                return carry
+
+            lax.fori_loop(0, layers, more, 0)
+            out_total = out_acc[...]
+        parts = hidden // LANES
+
+        def turn(i, carry):
+            at = pl.ds(pl.multiple_of(i * LANES, LANES), LANES)
+            rows_of = pl.ds(lax.rem(i, parts) * 2 + i // parts, width, stride=2 * parts)
+            total = self.whole[at, :] + in_part[0, at, :].astype(jnp.float32)
+            self.turned[rows_of, :] = total.T
+            return carry
+
+        lax.fori_loop(0, 2 * parts, turn, 0)
+        return out_total + out_part[0].astype(jnp.float32)
+
+
+def sums_scratch(layers, tokens, width, hidden):
+    low, full = jnp.bfloat16, jnp.float32
+    return [
+        pltpu.VMEM((layers * tokens, width + LANES), low),
+        pltpu.VMEM((layers, width, tokens), low),
+        pltpu.VMEM((layers, LANES // 2, tokens), full),
+        pltpu.VMEM((2 * hidden, width), full),
+        pltpu.VMEM((width * 2 * hidden // LANES, LANES), full),
+        pltpu.SemaphoreType.DMA((2,)),
+    ] + ([pltpu.VMEM((hidden, width), full)] if layers > 4 else [])
+
+
+def widened(turned, target):
+    size = target.shape[1] // 4
+
+    def piece(i, carry):
+        at = pl.ds(pl.multiple_of(i * size, size), size)
+        target[0, at, :] = turned[at, :].astype(target.dtype)
+        return carry
+
+    lax.fori_loop(0, 4, piece, 0)
+
+
+def cover_body(sizes, kinds, experts, first, in_ref, out_ref, in_part, out_part, rows_far, grads_far, *refs):
     count = len(kinds)
     sources, in_sum, out_sum = refs[:count], refs[count], refs[count + 1]
     targets = refs[count + 2 : 2 * count + 2]
-    rows, grads, weights, whole, turned, load_sem, *rest = refs[2 * count + 2 :]
-    sums, sems = rest[:-3], rest[-3:]
+    sums = Sums(*refs[2 * count + 2 : -3])
+    moves = Moves(sizes, kinds, sources, targets, refs[-3:])
     step = pl.program_id(0)
-    layers, width, tokens = grads.shape
-    hidden = out_ref.shape[1]
-    moves = Moves(sizes, kinds, sources, targets, sems)
 
     @pl.when(step == 0)
     def _():
-        loads = [
-            pltpu.make_async_copy(rows_far, rows, load_sem.at[0]),
-            pltpu.make_async_copy(grads_first, grads.at[pl.ds(0, 1)], load_sem.at[1]),
-            pltpu.make_async_copy(grads_second, grads.at[pl.ds(1, 1)], load_sem.at[2]),
-            pltpu.make_async_copy(grads_rest, grads.at[pl.ds(2, layers - 2)], load_sem.at[3]),
-        ]
+        loads = sums.loads(rows_far, grads_far)
         for load in loads:
             load.start()
         moves.barrier()
         moves.start()
         for load in loads:
             load.wait()
-        for i in range(layers):
-            weights[i] = weight_rows(rows[i * tokens : (i + 1) * tokens, width:])
+        sums.ready()
 
     index = lax.axis_index("row") * experts + first + step
-
-    def part_of(at, pieces):
-        block = rows[pl.ds(pl.multiple_of(at * tokens, tokens), pieces * tokens), :width]
-        weight = jnp.concatenate(
-            [weights[at + i, pl.ds(index, 1), :] for i in range(pieces)], axis=1
-        )
-        active_grad = jnp.concatenate(
-            [dot(out_ref[0], grads[at + i]) for i in range(pieces)], axis=1
-        )
-        active, gate_up_grad, _ = expert_terms(dot(in_ref[0], block, 0, 1), active_grad, weight)
-        out_total = functools.reduce(
-            jnp.add,
-            [
-                dot(active[:, i * tokens : (i + 1) * tokens], grads[at + i], 1, 1)
-                for i in range(pieces)
-            ],
-        )
-        return dot(gate_up_grad, block), out_total
-
-    if not sums:
-        in_total, out_total = part_of(0, layers)
-    else:
-        in_acc, out_acc = sums
-        in_acc[...] = jnp.zeros_like(in_acc)
-        out_acc[...] = jnp.zeros_like(out_acc)
-
-        def more(i, carry):
-            in_more, out_more = part_of(i, 1)
-            in_acc[...] += in_more
-            out_acc[...] += out_more
-            return carry
-
-        lax.fori_loop(0, layers, more, 0)
-        in_total, out_total = in_acc[...], out_acc[...]
-    whole[...] = in_total
-    parts = hidden // LANES
-
-    def turn(i, carry):
-        at = pl.ds(pl.multiple_of(i * LANES, LANES), LANES)
-        first = lax.rem(i, parts) * 2 + i // parts
-        rows_of = pl.ds(first, width, stride=2 * parts)
-        turned[rows_of, :] = (whole[at, :] + in_part[0, at, :].astype(jnp.float32)).T
-        return carry
-
-    lax.fori_loop(0, 2 * parts, turn, 0)
-
-    def narrow(i, carry):
-        at = pl.ds(pl.multiple_of(i * width, width), width)
-        in_sum[0, at, :] = turned[at, :].astype(jnp.bfloat16)
-        return carry
-
-    lax.fori_loop(0, 2 * parts, narrow, 0)
-    out_sum[0] = (out_total + out_part[0].astype(jnp.float32)).astype(jnp.bfloat16)
+    out_total = sums.make(index, in_ref[0], out_ref[0], in_part, out_part)
+    widened(sums.turned, in_sum)
+    out_sum[0] = out_total.astype(jnp.bfloat16)
 
     @pl.when(step == pl.num_programs(0) - 1)
     def _():
@@ -758,49 +853,59 @@
 
 
 def cover(sizes, name, number, first, count, work, *items):
-    w_in, w_out, in_part, out_part, rows_far, *grads_far = work
-    layers = sum(g.shape[0] for g in grads_far)
-    width, tokens = grads_far[0].shape[1:]
+    w_in, w_out, in_part, out_part, rows_far, grads_far = work
+    layers, width, tokens = grads_far.shape
     experts, hidden, _ = w_out.shape
     kinds, shapes, sems = planned(sizes, items)
     each = lambda s: pl.BlockSpec((1,) + s[1:], lambda e: (first + e, 0, 0))
     out = lambda s: pl.BlockSpec((1,) + s[1:], lambda e: (e, 0, 0))
-    turned = (width * 2 * hidden // LANES, LANES)
-    outs = [(count,) + turned, (count, hidden, width)]
-    sums = [(2 * hidden, width), (hidden, width)] if layers > 4 else []
+    outs = [(count, width * 2 * hidden // LANES, LANES), (count, hidden, width)]
     return pl.pallas_call(
         functools.partial(cover_body, sizes, kinds, experts, first),
         grid=(count,),
-        in_specs=[each(a.shape) for a in work[:4]] + [HBM] * (len(work) - 4 + len(items)),
+        in_specs=[each(a.shape) for a in work[:4]] + [HBM] * (2 + len(items)),
         out_specs=tuple(out(s) for s in outs) + (HBM,) * len(items),
         out_shape=tuple(jax.ShapeDtypeStruct(s, jnp.bfloat16) for s in outs) + tuple(shapes),
-        scratch_shapes=[
-            pltpu.VMEM(rows_far.shape, jnp.bfloat16),
-            pltpu.VMEM((layers, width, tokens), jnp.bfloat16),
-            pltpu.VMEM((layers, LANES // 2, tokens), jnp.float32),
-            pltpu.VMEM((2 * hidden, width), jnp.float32),
-            pltpu.VMEM(turned, jnp.float32),
-            pltpu.SemaphoreType.DMA((1 + len(grads_far),)),
-        ]
-        + [pltpu.VMEM(s, jnp.float32) for s in sums]
-        + sems,
+        scratch_shapes=sums_scratch(layers, tokens, width, hidden) + sems,
         compiler_params=pltpu.CompilerParams(collective_id=number, has_side_effects=True),
         name=name,
     )(*work, *[item[1] for item in items])
 
 
-def outputs_body(counts, *refs):
-    pieces = len(counts)
+def order_of(total, late):
+    if not late:
+        return list(range(total))
+    share = (total - late) // late
+    order = []
+    for i in range(late):
+        order += list(range(i * share, (i + 1) * share)) + [total - late + i]
+    return order
+
+
+def picked(values, step):
+    chosen = values[0]
+    for i, value in enumerate(values[1:], 1):
+        if value != values[i - 1]:
+            chosen = jnp.where(step >= i, value, chosen)
+    return chosen
+
+
+def outputs_body(counts, order, *refs):
+    pieces, late = len(counts), len(order) - sum(counts)
     in_sums, out_sums = refs[:pieces], refs[pieces : 2 * pieces]
-    blocks, in_blocks, gains, sums, output_all = refs[2 * pieces : 2 * pieces + 5]
-    gin, gout, block_out, in_grad, gain_attn, gain_moe, query, pair, output, router = refs[
-        2 * pieces + 5 :
-    ]
+    refs = refs[2 * pieces :]
+    blocks, in_blocks, gains, sums_all, output_all = refs[:5]
+    work, refs = (refs[5:11], refs[11:]) if late else ((), refs[5:])
+    gin, gout, block_out, in_grad, gain_attn, gain_moe, query, pair, output, router = refs[:10]
+    sums = Sums(*refs[10:]) if late else None
     step = pl.program_id(0)
     width = gout.shape[2]
 
     @pl.when(step == 0)
     def _():
+        if late:
+            for load in sums.loads(*work[4:]):
+                load.start()
         for i in range(blocks.shape[0]):
             at = pl.ds(i * blocks.shape[1], blocks.shape[1])
             block_out[at, :] = blocks[i]
@@ -808,45 +913,75 @@
         gain_sum = jnp.sum(gains[...], axis=0)
         gain_attn[...] = gain_sum[0:1, :]
         gain_moe[...] = gain_sum[1:2, :]
-        query[...] = sums[:width, :].astype(jnp.float32)
-        pair[...] = sums[width : 2 * width, :].astype(jnp.float32)
+        query[...] = sums_all[:width, :].astype(jnp.float32)
+        pair[...] = sums_all[width : 2 * width, :].astype(jnp.float32)
         for i in range(width // LANES):
             at = slice(i * LANES, (i + 1) * LANES)
             output[:, at] = output_all[at, :].astype(jnp.float32)
-        router[...] = sums[2 * width : 2 * width + router.shape[0], :].astype(jnp.float32)
-
+        router[...] = sums_all[2 * width : 2 * width + router.shape[0], :].astype(jnp.float32)
+
+    expert = picked(order, step)
     first = 0
     for count, in_sum, out_sum in zip(counts, in_sums, out_sums):
 
-        @pl.when((step >= first) & (step < first + count))
+        @pl.when((expert >= first) & (expert < first + count))
         def _(in_sum=in_sum, out_sum=out_sum):
             gout[0] = out_sum[0].astype(jnp.float32)
-            gin[0] = in_sum[0].astype(jnp.float32)
+            widened(in_sum.at[0], gin)
 
         first += count
-
-
-def outputs(in_sums, out_sums, hidden, blocks, in_blocks, gains, sums, output_all, experts):
+    if late:
+
+        @pl.when(expert >= first)
+        def _():
+            @pl.when(expert == first)
+            def _():
+                for load in sums.loads(*work[4:]):
+                    load.wait()
+                sums.ready()
+
+            index = lax.axis_index("row") * len(order) + expert
+            gout[0] = sums.make(index, work[0][0], work[1][0], *work[2:4])
+            widened(sums.turned, gin)
+
+
+def outputs(in_sums, out_sums, work, blocks, in_blocks, gains, sums, output_all, experts):
+    w_out, grads_far = work[1], work[5]
+    total, hidden, width = w_out.shape
+    layers, _, tokens = grads_far.shape
     counts = [s.shape[0] for s in in_sums]
-    width = out_sums[0].shape[2]
+    late = total - sum(counts)
+    order = order_of(total, late)
     parts = hidden // LANES
-    group, own, lanes = blocks.shape
-    tokens = group * own
+    lanes = blocks.shape[2]
     once = lambda s: pl.BlockSpec(s, lambda e: (0,) * len(s))
-    each = lambda s: pl.BlockSpec((1,) + s[1:], lambda e: (e, 0, 0))
+    each = lambda s: pl.BlockSpec((1,) + s[1:], lambda e: (picked(order, e), 0, 0))
     specs = []
     for arrays in (in_sums, out_sums):
         first = 0
         for array in arrays:
-            count = array.shape[0]
+            places, last = [], 0
+            for expert in order:
+                if first <= expert < first + array.shape[0]:
+                    last = expert - first
+                elif expert < total - late and expert >= first + array.shape[0]:
+                    last = array.shape[0] - 1
+                places.append(last)
             specs.append(
                 pl.BlockSpec(
-                    (1,) + array.shape[1:],
-                    lambda e, first=first, count=count: (jnp.clip(e - first, 0, count - 1), 0, 0),
+                    (1,) + array.shape[1:], lambda e, places=places: (picked(places, e), 0, 0)
                 )
             )
-            first += count
-    total = sum(counts)
+            first += array.shape[0]
+    more, scratch = (), []
+    if late:
+        turns, place = [], total - late
+        for expert in order:
+            turns.append(place)
+            place = min(place + (expert >= total - late), total - 1)
+        ahead = lambda s: pl.BlockSpec((1,) + s[1:], lambda e: (picked(turns, e), 0, 0))
+        more = work
+        scratch = sums_scratch(layers, tokens, width, hidden)
     full = jnp.float32
     shapes = [
         ((total, width * 2 * parts, LANES), full),
@@ -860,14 +995,19 @@
         ((LANES, width), full),
         ((experts, LANES), full),
     ]
+    small = (blocks, in_blocks, gains, sums, output_all)
     gin, *others = pl.pallas_call(
-        functools.partial(outputs_body, counts),
+        functools.partial(outputs_body, counts, order),
         grid=(total,),
-        in_specs=specs + [once(a.shape) for a in (blocks, in_blocks, gains, sums, output_all)],
+        in_specs=specs
+        + [once(a.shape) for a in small]
+        + [ahead(a.shape) for a in more[:4]]
+        + [HBM for _ in more[4:]],
         out_specs=(each(shapes[0][0]), each(shapes[1][0])) + tuple(once(s) for s, _ in shapes[2:]),
         out_shape=tuple(jax.ShapeDtypeStruct(*shape) for shape in shapes),
+        scratch_shapes=scratch,
         name="outputs",
-    )(*in_sums, *out_sums, blocks, in_blocks, gains, sums, output_all)
+    )(*in_sums, *out_sums, *small, *more)
     gin = gin.reshape(total, width, parts, 2, LANES).transpose(0, 1, 3, 2, 4)
     return gin.reshape(total, width, 2, hidden), *others
 
@@ -899,7 +1039,6 @@
     low, full = jnp.bfloat16, jnp.float32
     layer = lax.axis_index("dp")
     me = lax.axis_index("row") * cols + lax.axis_index("col")
-    everyone = list(range(1, depth))
     hops = list(range(1, hop_count + 1))
 
     tokens_blocks, gains, router, docs_far, grads_shifted, grad_blocks = exchange(
@@ -907,10 +1046,10 @@
         "gather_tokens",
         0,
         ("gather", tokens, False, 2),
-        ("gather", jnp.stack([gain_attn, gain_moe])),
-        ("gather", w_router.T),
-        ("shift", doc_ids.reshape(-1, LANES), everyone, False),
-        ("shift", out_grad, everyone, False),
+        ("share", jnp.stack([gain_attn, gain_moe])),
+        ("share", w_router.T),
+        ("line", doc_ids.reshape(-1, LANES), False),
+        ("line", out_grad, False),
         ("gather", out_grad, False, 2),
     )
 
@@ -952,7 +1091,7 @@
 
     stack = (hop_count + 1,) + block
     twice = (2 * tok_rows, LANES)
-    mixed, log_total, start, grads_first = hosted(
+    mixed, log_total, start = call(
         attend_body,
         "attend",
         [(block, low), ((2 * tok_rows, 1), full), ((tok_rows, 1), jnp.int32)],
@@ -967,9 +1106,6 @@
             pltpu.VMEM(twice, low),
             pltpu.VMEM(twice, full),
         ],
-        sizes=sizes,
-        number=10,
-        items=[("gather", far_turned[:1], True)],
     )
     (mixed_own,) = exchange(
         sizes, "swap_mixed", 2, ("swap", mixed.reshape(group, own, LANES))
@@ -986,13 +1122,8 @@
         expert_ids.T,
         scratch=[pltpu.VMEM(expert_ids.shape, full)],
     )
-    rows_blocks, rows_shifted, grads_second = exchange(
-        sizes,
-        "gather_rows",
-        3,
-        ("gather", rows_own, False, 2),
-        ("shift", rows_own, everyone, False),
-        ("gather", far_turned[1:2], True),
+    rows_blocks, rows_shifted = exchange(
+        sizes, "gather_rows", 3, ("gather", rows_own, False, 2), ("line", rows_own, False)
     )
     rows_near = rows_blocks.reshape(tok_rows, -1)
     parts = hidden // LANES
@@ -1005,14 +1136,12 @@
         grads_near.reshape(width, tok_rows),
         in_rows,
         w_expert_out,
-        far_turned[2:],
+        far_turned,
         rows_shifted,
     )
     rows_far = rows_far.reshape((depth - 1) * tok_rows, -1)
-    grads_far = [
-        g.reshape(-1, width, tok_rows) for g in (grads_first, grads_second, grads_far)
-    ]
-    work = (in_flat, w_expert_out, in_part, out_part, rows_far, *grads_far)
+    grads_far = grads_far.reshape(depth - 1, width, tok_rows)
+    work = (in_flat, w_expert_out, in_part, out_part, rows_far, grads_far)
     share = expert_local // 4
     unit = 16 * depth
     in_sums, out_sums = [], []
@@ -1104,12 +1233,11 @@
         gains,
         gain_moe_part,
     )
-    partial_blocks, sums_turned, output_all, gain_blocks = beneath(
+    partial_blocks, sums_turned, gain_blocks = beneath(
         "swap_partial",
         7,
         ("swap", partial.reshape(group, own, width)),
         ("turn", sums.reshape(depth, length // depth, LANES)),
-        ("collect", output_summed),
         ("swap", gain_parts),
     )
     pieces = (group, own, LANES)
@@ -1131,18 +1259,22 @@
         gain_blocks,
         sums_turned,
     )
-    block_out, in_grad, gain_all, sums = beneath(
-        "swap_results",
-        8,
+    results = [
         ("swap", block_out),
         ("swap", in_grad),
-        ("collect", gain_sum),
-        ("collect", summed),
-    )
+        ("line", gain_sum, True),
+        ("line", summed, True),
+        ("line", output_summed, True),
+    ]
+    if depth > 4:
+        moved = beneath("swap_results", 8, *results)
+    else:
+        moved = exchange(sizes, "swap_results", 8, *results)
+    block_out, in_grad, gain_all, sums, output_all = moved
     grad_in, grad_out, block_out, in_grad, gain_attn_sum, gain_moe_sum, query_sum, pair_sum, output_sum, router_sum = outputs(
         in_sums,
         out_sums,
-        hidden,
+        work,
         block_out,
         in_grad,
         gain_all,

time: 259 us -> 270 us (1.042)
  Pallas kernels: 253 us -> 265 us
    pallas_call x4 -> x3, Pallas kernels: 85.2 us -> 60.2 us  [cover(): pl.pallas_call(functools.partial(cover_body, sizes, kinds, experts, first...]
    pallas_call x5 -> x6, Pallas kernels: 74.5 us -> 90.2 us  [exchange(): pl.pallas_call(functools.partial(exchange_body, sizes, kinds), out_shape=...]
    pallas_call x1, Pallas kernels: 35.2 us -> 49.6 us  [local_experts(): pl.pallas_call(functools.partial(local_experts_body, sizes, kinds), grid=...]
    pallas_call x6 -> x7, Pallas kernels: 28.8 us -> 35.4 us  [call(): pl.pallas_call(body, out_shape=tuple((jax.ShapeDtypeStruct(*shape) for sh...]
    pallas_call x2 -> x1, Pallas kernels: 29.1 us -> 30 us  [outputs(): pl.pallas_call(functools.partial(outputs_body, counts, order), grid=(tota...]
where the time goes in v1:
time: 270 us; the launch traced here: 269 us
  Pallas kernels  265 us (98%)
  other arithmetic  3.03 us (1%)
    pallas_call x6, Pallas kernels, exchange(): pl.pallas_call(functools.partial(exchange_body, sizes, kinds), out_shape=...  90.2 us
    pallas_call x3, Pallas kernels, cover(): pl.pallas_call(functools.partial(cover_body, sizes, kinds, experts, first...  60.2 us
    pallas_call x1, Pallas kernels, local_experts(): pl.pallas_call(functools.partial(local_experts_body, sizes, kinds), grid=...  49.6 us
    pallas_call x7, Pallas kernels, call(): pl.pallas_call(body, out_shape=tuple((jax.ShapeDtypeStruct(*shape) for sh...  35.4 us
    pallas_call x1, Pallas kernels, outputs(): pl.pallas_call(functools.partial(outputs_body, counts, order), grid=(tota...  30 us

profile of v1, /device:TPU:0, one launch (start us, length us, event | category | flops | bytes accessed | tf_op | source)
XLA Modules:
  0.0 269.4 jit_solution(10672947218452242642)
XLA Ops:
  0.6 1.2 pad_maximum_fusion.refs_1_
  1.9 1.8 fusion
  3.7 22.4 %gather_tokens.1 = (bf16[8,512,128]{2,1,0:T(8,128)(2,1)}, bf16[8,2,128]{2,1,0:T(2,128)(2,1)}, bf16[8,32,128]{2,1,0:T(8,128)(2,1)}, s32[3,4,128]{2,1,0:T(4,128)},...) custom-call(bf16[512,128]{1,0:T(8,128)(2,1)} %refs_0_.1, bf16[2,128]{1,0:T(2,128)(2,1)} %pad_maximum_fusion.refs_1_, ...), custom_call_target="tpu_custom_call" | custom-call | tf_op jit(solution)/shard_map/gather_tokens/pallas_call | solution.py:296
  26.1 4.4 %project.1 = (bf16[512,1024]{1,0:T(8,128)(2,1)}, bf16[512,128]{1,0:T(8,128)(2,1)}, bf16[512,128]{1,0:T(8,128)(2,1)}, bf16[64,1024]{1,0:T(8,128)(2,1)}, bf16[64,1...) custom-call(bf16[8,512,128]{2,1,0:T(8,128)(2,1)} %get-tuple-element.86.blocks, ...), custom_call_target="tpu_custom_call" | custom-call | tf_op jit(solution)/shard_map/project/pallas_call | solution.py:318
  30.5 14.5 %shift_pairs.1 = (bf16[2,512,128]{2,1,0:T(8,128)(2,1)}, bf16[8,128,1024]{2,1,0:T(8,128)(2,1)}) custom-call(bf16[512,128]{1,0:T(8,128)(2,1)} %get-tuple-element.91.refs_0_.pair, bf16[128,1024]{1,0:T(8,128)(2,1)} %w_output.1), custom_call_target="tpu_custom_call" | custom-call | tf_op jit(solution)/shard_map/shift_pairs/pallas_call | solution.py:296
  45.0 6.5 %attend.1 = (bf16[512,128]{1,0:T(8,128)(2,1)}, f32[1024,1]{1,0:T(8,128)}, s32[512,1]{1,0:T(8,128)}) custom-call(bf16[512,128]{1,0:T(8,128)(2,1)} %get-tuple-element.90.query, bf16[512,128]{1,0:T(8,128)(2,1)} %get-tuple-element.91.refs_0_.pair, bf16[2,512,128]{2,1,0:T(8,128)(2,1)} %get-tuple-element.92.far, s32[4,128]{1,0:T(4,128)} %bitcast.64, ...), custom_call_target="tpu_custom_call" | custom-call | tf_op jit(solution)/shard_map/attend/pallas_call | solution.py:318
  51.5 5.9 %swap_mixed.1.mixed = bf16[8,64,128]{2,1,0:T(8,128)(2,1)} custom-call(bf16[8,64,128]{2,1,0:T(8,128)(2,1)} %bitcast.58), custom_call_target="tpu_custom_call" | custom-call | tf_op jit(solution)/shard_map/swap_mixed/pallas_call | solution.py:296
  57.4 3.9 %middle.1 = (bf16[64,1152]{1,0:T(8,128)(2,1)}, f32[64,1024]{1,0:T(8,128)}, f32[64,128]{1,0:T(8,128)}) custom-call(bf16[8,64,128]{2,1,0:T(8,128)(2,1)} %swap_mixed.1.mixed, bf16[64,1024]{1,0:T(8,128)(2,1)} %get-tuple-element.95.own, bf16[1024,1024]{1,0:T(8,128)(2,1)} %bitcast.48, bf16[8,2,128]{2,1,0:T(2,128)(2,1)} %get-tuple-element.87.gains, ...), custom_call_target="tpu_custom_call" | custom-call | tf_op jit(solution)/shard_map/middle/pallas_call | solution.py:318
  61.3 15.8 %gather_rows.1 = (bf16[8,64,1152]{2,1,0:T(8,128)(2,1)}, bf16[3,64,1152]{2,1,0:T(8,128)(2,1)}) custom-call(bf16[64,1152]{1,0:T(8,128)(2,1)} %get-tuple-element.98.refs_0_.refs_1_, bf16[64,1152]{1,0:T(8,128)(2,1)} %get-tuple-element.98.refs_0_.refs_1_), custom_call_target="tpu_custom_call" | custom-call | tf_op jit(solution)/shard_map/gather_rows/pallas_call | solution.py:296
  77.1 49.6 %local_experts.1 = (bf16[512,1024]{1,0:T(8,128)(2,1)}, bf16[512,1152]{1,0:T(8,128)(2,1)}, bf16[8,1024,512]{2,1,0:T(8,128)(2,1)}, bf16[8,512,1024]{2,1,0:T(8,128)...) custom-call(bf16[512,1152]{1,0:T(8,128)(2,1)} %bitcast.46, ...), custom_call_target="tpu_custom_call" | custom-call | tf_op jit(solution)/shard_map/local_experts/pallas_call | solution.py:709
  126.7 19.6 %swap_back.1 = (bf16[2,4096,128]{2,1,0:T(8,128)(2,1)}, bf16[2,256,1024]{2,1,0:T(8,128)(2,1)}, bf16[8,64,1152]{2,1,0:T(8,128)(2,1)}) custom-call(bf16[8,1024,512]{2,1,0:T(8,128)(2,1)} %get-tuple-element.103.in_ref.refs_11_, bf16[8,256,1024]{2,1,0:T(8,128)(2,1)} %refs_12_.1, bf16[8,512,1024]{2,1,0:T(8,128)(2,1)} %get-tuple-element.104.in_part.refs_13_, ...), custom_call_target="tpu_custom_call" | custom-call | tf_op jit(solution)/shard_map/swap_back/pallas_call | solution.py:863
  146.3 2.7 %middle_back.1 = (f32[64,1024]{1,0:T(8,128)}, bf16[64,1024]{1,0:T(8,128)(2,1)}, bf16[64,128]{1,0:T(8,128)(2,1)}, f32[1,1024]{1,0:T(1,128)}) custom-call(bf16[8,64,1152]{2,1,0:T(8,128)(2,1)} %get-tuple-element.110.back, bf16[64,1024]{1,0:T(8,128)(2,1)} %get-tuple-element.111.out_grad, f32[64,1024]{1,0:T(8,128)} %get-tuple-element.112.middle, ...), custom_call_target="tpu_custom_call" | custom-call | tf_op jit(solution)/shard_map/middle_back/pallas_call | solution.py:318
  149.0 13.2 %gather_attn_grad.1 = (bf16[8,64,1024]{2,1,0:T(8,128)(2,1)}, bf16[8,64,128]{2,1,0:T(8,128)(2,1)}) custom-call(bf16[64,1024]{1,0:T(8,128)(2,1)} %get-tuple-element.114.refs_0_, bf16[64,128]{1,0:T(8,128)(2,1)} %get-tuple-element.115.refs_1_), custom_call_target="tpu_custom_call" | custom-call | tf_op jit(solution)/shard_map/gather_attn_grad/pallas_call | solution.py:296
  162.2 10.4 %attend_back.1 = (bf16[512,128]{1,0:T(8,128)(2,1)}, f32[512,128]{1,0:T(8,128)}, bf16[2,512,128]{2,1,0:T(8,128)(2,1)}, bf16[8,128,128]{2,1,0:T(8,128)(2,1)}) custom-call(bf16[512,1024]{1,0:T(8,128)(2,1)} %bitcast.53, bf16[128,1024]{1,0:T(8,128)(2,1)} %w_output.1, bf16[512,128]{1,0:T(8,128)(2,1)} %get-tuple-element.90.query, ...), custom_call_target="tpu_custom_call" | custom-call | tf_op jit(solution)/shard_map/attend_back/pallas_call | solution.py:318
  172.6 20.7 %shift_grads.1 = (bf16[2,4096,128]{2,1,0:T(8,128)(2,1)}, bf16[2,256,1024]{2,1,0:T(8,128)(2,1)}, bf16[2,512,128]{2,1,0:T(8,128)(2,1)}, bf16[8,64,1024]{2,1,0:T(8,128)(2,1)}, bf16[4,256,128]{2,1,0:T(8,128)(2,1)}) custom-call(bf16[8,1024,512]{2,1,0:T(8,128)(2,1)} %get-tuple-element.103.in_ref.refs_11_, bf16[8,256,1024]{2,1,0:T(8,128)(2,1)} %refs_12_.1, ...), custom_call_target="tpu_custom_call" | custom-call | tf_op jit(solution)/shard_map/shift_grads/pallas_call | solution.py:863
  193.3 4.4 %project_back.1 = (bf16[512,1024]{1,0:T(8,128)(2,1)}, bf16[2176,128]{1,0:T(8,128)(2,1)}, bf16[256,128]{1,0:T(8,128)(2,1)}, f32[8,8,128]{2,1,0:T(8,128)}) custom-call(bf16[512,128]{1,0:T(8,128)(2,1)} %get-tuple-element.123.query_grad, f32[512,128]{1,0:T(8,128)} %get-tuple-element.124.pair_grad, bf16[2,512,128]{2,1,0:T(8,128)(2,1)} %get-tuple-element.125.returned, ...), custom_call_target="tpu_custom_call" | custom-call | tf_op jit(solution)/shard_map/project_back/pallas_call | solution.py:318
  197.8 19.9 %swap_partial.1 = (bf16[2,4096,128]{2,1,0:T(8,128)(2,1)}, bf16[2,256,1024]{2,1,0:T(8,128)(2,1)}, bf16[8,64,1024]{2,1,0:T(8,128)(2,1)}, bf16[4,544,128]{2,1,0:T(8,128)(2,1)}, f32[8,8,128]{2,1,0:T(8,128)}) custom-call(bf16[8,1024,512]{2,1,0:T(8,128)(2,1)} %get-tuple-element.103.in_ref.refs_11_, bf16[8,256,1024]{2,1,0:T(8,128)(2,1)} %refs_12_.1, ...), custom_call_target="tpu_custom_call" | custom-call | tf_op jit(solution)/shard_map/swap_partial/pallas_call | solution.py:863
  217.7 3.1 %results.1 = (bf16[8,64,128]{2,1,0:T(8,128)(2,1)}, bf16[8,64,128]{2,1,0:T(8,128)(2,1)}, f32[8,128]{1,0:T(8,128)}, bf16[544,128]{1,0:T(8,128)(2,1)}) custom-call(bf16[8,64,1024]{2,1,0:T(8,128)(2,1)} %get-tuple-element.137.blocks, bf16[8,64,1024]{2,1,0:T(8,128)(2,1)} %get-tuple-element.138.moe, bf16[64,1024]{1,0:T(8,128)(2,1)} %get-tuple-element.95.own, ...), custom_call_target="tpu_custom_call" | custom-call | tf_op jit(solution)/shard_map/results/pallas_call | solution.py:318
  220.8 18.4 %swap_results.1 = (bf16[8,64,128]{2,1,0:T(8,128)(2,1)}, bf16[8,64,128]{2,1,0:T(8,128)(2,1)}, f32[4,8,128]{2,1,0:T(8,128)}, bf16[4,544,128]{2,1,0:T(8,128)(2,1)}, bf16[4,256,128]{2,1,0:T(8,128)(2,1)}) custom-call(bf16[8,64,128]{2,1,0:T(8,128)(2,1)} %get-tuple-element.142.refs_0_, bf16[8,64,128]{2,1,0:T(8,128)(2,1)} %get-tuple-element.143.refs_1_, ...), custom_call_target="tpu_custom_call" | custom-call | tf_op jit(solution)/shard_map/swap_results/pallas_call | solution.py:296
  239.2 30.0 %outputs.1 = (f32[8,4096,128]{2,1,0:T(8,128)}, f32[8,256,1024]{2,1,0:T(8,128)}, bf16[512,128]{1,0:T(8,128)(2,1)}, bf16[512,128]{1,0:T(8,128)(2,1)}, f32[1,128]{1...) custom-call(bf16[2,4096,128]{2,1,0:T(8,128)(2,1)} %get-tuple-element, ...), custom_call_target="tpu_custom_call" | custom-call | tf_op jit(solution)/shard_map/outputs/pallas_call | solution.py:999
  (2 shorter events, 0.0 us)

commit v2 on v1

--- a/solution.py
+++ b/solution.py
@@ -61,7 +61,7 @@
             if kind[0] == "shift":
                 for d in kind[1]:
                     shifts |= {d % depth, -d % depth}
-            elif kind[0] == "turn":
+            elif kind[0] in ("turn", "collect"):
                 shifts |= set(range(1, depth))
         for k in sorted(shifts - {0}):
             partners.append({"dp": lax.rem(layer + k, depth)})
@@ -153,10 +153,10 @@
                         ways.append((near, piece, first, onward))
                     for near, piece, first, onward in ways:
                         nexts = [onward] + to_mates(at(near, part))
-                        follow.append((2 + 3 * part, None, first[1], nexts))
+                        follow.append((2 + 3 * part, 0, None, first[1], nexts))
                     for near, piece, first, onward in ways:
                         nexts = to_mates(at(away, part, piece))
-                        follow.append((2 + 3 * parts + part, None, onward[1], nexts))
+                        follow.append((2 + 3 * parts + part, 1, None, onward[1], nexts))
                     for j in range(1, cols):
                         direct(some, at(row, part), {"col": lax.rem(col + j, cols)})
                 keep(source, target.at[:, me] if second else target.at[me])
@@ -166,11 +166,12 @@
                     piece = source.at[other] if kind[0] == "swap" else source
                     direct(piece, target.at[me], self.member(other))
                 keep(source.at[me] if kind[0] == "swap" else source, target.at[me])
-            elif kind[0] == "turn":
+            elif kind[0] in ("turn", "collect"):
                 for k in range(1, depth):
                     other = lax.rem(layer + k, depth)
-                    direct(source.at[other], target.at[layer], {"dp": other})
-                keep(source.at[layer], target.at[layer])
+                    piece = source.at[other] if kind[0] == "turn" else source
+                    direct(piece, target.at[layer], {"dp": other})
+                keep(source.at[layer] if kind[0] == "turn" else source, target.at[layer])
             elif kind[0] == "line":
                 absolute = kind[1]
                 for way in (1, -1):
@@ -198,7 +199,7 @@
                         block = held(step, layer)
                         arrival = remote(block, block, {"dp": onward}, mine[step - 1])
                         nexts = [(more, sending(step + 1))] if step + 1 < depth else []
-                        follow.append((4 * step, behind >= step, arrival, nexts))
+                        follow.append((4 * step, 0, behind >= step, arrival, nexts))
                 if absolute:
                     keep(source, target.at[layer])
             else:
@@ -226,8 +227,10 @@
         for copy in local:
             copy().start()
 
-    def relay(self, only=None):
-        for _, condition, copy, nexts in self.plan(only)[1]:
+    def relay(self, only=None, stage=None):
+        for _, at, condition, copy, nexts in self.plan(only)[1]:
+            if stage is not None and stage != at:
+                continue
 
             def action(copy=copy, nexts=nexts):
                 copy().wait_recv()
@@ -270,9 +273,9 @@
             copies += 2 * (depth - 1)
         else:
             kinds.append((name,))
-            if name == "share":
-                shape = (group,) + shape
-            copies += (depth if name == "turn" else group) - 1
+            if name in ("share", "collect"):
+                shape = (group if name == "share" else depth,) + shape
+            copies += (depth if name in ("turn", "collect") else group) - 1
         shapes.append(jax.ShapeDtypeStruct(shape, array.dtype))
     sems = [
         pltpu.SemaphoreType.DMA((copies,)),
@@ -652,9 +655,11 @@
         share[...] = jnp.zeros_like(share)
         weights[...] = weight_rows(rows_ref[:, width:])
 
-    @pl.when(step == steps // 2)
-    def _():
-        moves.relay([0])
+    for when, item, stage in ((3, 0, 0), (5, 1, 0), (7, 0, 1)):
+
+        @pl.when(step == when * steps // 8)
+        def _(item=item, stage=stage):
+            moves.relay([item], stage)
 
     for i in range(each):
         spread[i] = in_ref[i].astype(jnp.float32)
@@ -681,7 +686,7 @@
         moe_ref[...] = moe_acc[...].astype(jnp.bfloat16)
         back_ref[:, :width] = back_acc[...].astype(jnp.bfloat16)
         back_ref[:, width:] = share[...].T.astype(jnp.bfloat16)
-        moves.relay([1])
+        moves.relay([1], 1)
         moves.finish()
 
 
@@ -791,12 +796,12 @@
         def turn(i, carry):
             at = pl.ds(pl.multiple_of(i * LANES, LANES), LANES)
             rows_of = pl.ds(lax.rem(i, parts) * 2 + i // parts, width, stride=2 * parts)
-            total = self.whole[at, :] + in_part[0, at, :].astype(jnp.float32)
+            total = self.whole[at, :] + in_part[at, :].astype(jnp.float32)
             self.turned[rows_of, :] = total.T
             return carry
 
         lax.fori_loop(0, 2 * parts, turn, 0)
-        return out_total + out_part[0].astype(jnp.float32)
+        return out_total + out_part[...].astype(jnp.float32)
 
 
 def sums_scratch(layers, tokens, width, hidden):
@@ -811,45 +816,59 @@
     ] + ([pltpu.VMEM((hidden, width), full)] if layers > 4 else [])
 
 
-def widened(turned, target):
-    size = target.shape[1] // 4
+def widened(source, target):
+    size = target.shape[0] // 4
 
     def piece(i, carry):
         at = pl.ds(pl.multiple_of(i * size, size), size)
-        target[0, at, :] = turned[at, :].astype(target.dtype)
+        target[at, :] = source[at, :].astype(target.dtype)
         return carry
 
     lax.fori_loop(0, 4, piece, 0)
 
 
-def cover_body(sizes, kinds, experts, first, in_ref, out_ref, in_part, out_part, rows_far, grads_far, *refs):
+def cover_body(sizes, kinds, experts, first, *refs):
     count = len(kinds)
-    sources, in_sum, out_sum = refs[:count], refs[count], refs[count + 1]
-    targets = refs[count + 2 : 2 * count + 2]
-    sums = Sums(*refs[2 * count + 2 : -3])
+    work, sources = refs[:6], refs[6 : 6 + count]
+    in_sum, out_sum = refs[6 + count : 8 + count]
+    targets, refs = refs[8 + count : 8 + 2 * count], refs[8 + 2 * count :]
+    parts, made, part_sem, made_sem = refs[:4], refs[4:6], refs[6], refs[7]
+    sums = Sums(*refs[8:-3])
     moves = Moves(sizes, kinds, sources, targets, refs[-3:])
-    step = pl.program_id(0)
-
-    @pl.when(step == 0)
-    def _():
-        loads = sums.loads(rows_far, grads_far)
-        for load in loads:
-            load.start()
-        moves.barrier()
-        moves.start()
-        for load in loads:
-            load.wait()
-        sums.ready()
-
-    index = lax.axis_index("row") * experts + first + step
-    out_total = sums.make(index, in_ref[0], out_ref[0], in_part, out_part)
-    widened(sums.turned, in_sum)
-    out_sum[0] = out_total.astype(jnp.bfloat16)
-
-    @pl.when(step == pl.num_programs(0) - 1)
-    def _():
-        moves.relay()
-        moves.finish()
+    many = made[0].shape[0]
+    loads = [
+        pltpu.make_async_copy(source.at[pl.ds(first, many)], part, part_sem.at[i])
+        for i, (source, part) in enumerate(zip(work[:4], parts))
+    ] + sums.loads(*work[4:])
+    for load in loads[4:] + loads[:4]:
+        load.start()
+    moves.barrier()
+    moves.start()
+    for load in loads:
+        load.wait()
+    sums.ready()
+
+    def stores(i):
+        return [
+            pltpu.make_async_copy(made[0].at[i], in_sum.at[i], made_sem.at[i]),
+            pltpu.make_async_copy(made[1].at[i], out_sum.at[i], made_sem.at[many + i]),
+        ]
+
+    def expert(i, carry):
+        index = lax.axis_index("row") * experts + first + i
+        out_total = sums.make(index, parts[0][i], parts[1][i], parts[2].at[i], parts[3].at[i])
+        widened(sums.turned, made[0].at[i])
+        made[1][i] = out_total.astype(jnp.bfloat16)
+        for store in stores(i):
+            store.start()
+        return carry
+
+    lax.fori_loop(0, many, expert, 0)
+    moves.relay()
+    moves.finish()
+    for i in range(many):
+        for store in stores(i):
+            store.wait()
 
 
 def cover(sizes, name, number, first, count, work, *items):
@@ -857,55 +876,34 @@
     layers, width, tokens = grads_far.shape
     experts, hidden, _ = w_out.shape
     kinds, shapes, sems = planned(sizes, items)
-    each = lambda s: pl.BlockSpec((1,) + s[1:], lambda e: (first + e, 0, 0))
-    out = lambda s: pl.BlockSpec((1,) + s[1:], lambda e: (e, 0, 0))
+    low = jnp.bfloat16
     outs = [(count, width * 2 * hidden // LANES, LANES), (count, hidden, width)]
     return pl.pallas_call(
         functools.partial(cover_body, sizes, kinds, experts, first),
-        grid=(count,),
-        in_specs=[each(a.shape) for a in work[:4]] + [HBM] * (2 + len(items)),
-        out_specs=tuple(out(s) for s in outs) + (HBM,) * len(items),
-        out_shape=tuple(jax.ShapeDtypeStruct(s, jnp.bfloat16) for s in outs) + tuple(shapes),
-        scratch_shapes=sums_scratch(layers, tokens, width, hidden) + sems,
+        in_specs=[HBM] * (6 + len(items)),
+        out_specs=(HBM,) * (2 + len(items)),
+        out_shape=tuple(jax.ShapeDtypeStruct(s, low) for s in outs) + tuple(shapes),
+        scratch_shapes=[pltpu.VMEM((count,) + a.shape[1:], low) for a in work[:4]]
+        + [pltpu.VMEM(s, low) for s in outs]
+        + [pltpu.SemaphoreType.DMA((4,)), pltpu.SemaphoreType.DMA((2 * count,))]
+        + sums_scratch(layers, tokens, width, hidden)
+        + sems,
         compiler_params=pltpu.CompilerParams(collective_id=number, has_side_effects=True),
         name=name,
     )(*work, *[item[1] for item in items])
 
 
-def order_of(total, late):
-    if not late:
-        return list(range(total))
-    share = (total - late) // late
-    order = []
-    for i in range(late):
-        order += list(range(i * share, (i + 1) * share)) + [total - late + i]
-    return order
-
-
-def picked(values, step):
-    chosen = values[0]
-    for i, value in enumerate(values[1:], 1):
-        if value != values[i - 1]:
-            chosen = jnp.where(step >= i, value, chosen)
-    return chosen
-
-
-def outputs_body(counts, order, *refs):
-    pieces, late = len(counts), len(order) - sum(counts)
+def outputs_body(counts, *refs):
+    pieces = len(counts)
     in_sums, out_sums = refs[:pieces], refs[pieces : 2 * pieces]
-    refs = refs[2 * pieces :]
-    blocks, in_blocks, gains, sums_all, output_all = refs[:5]
-    work, refs = (refs[5:11], refs[11:]) if late else ((), refs[5:])
-    gin, gout, block_out, in_grad, gain_attn, gain_moe, query, pair, output, router = refs[:10]
-    sums = Sums(*refs[10:]) if late else None
+    blocks, in_blocks, gains, sums, output_all = refs[2 * pieces : 2 * pieces + 5]
+    gin, gout, *others = refs[2 * pieces + 5 :]
+    block_out, in_grad, gain_attn, gain_moe, query, pair, output, router = others
     step = pl.program_id(0)
     width = gout.shape[2]
 
     @pl.when(step == 0)
     def _():
-        if late:
-            for load in sums.loads(*work[4:]):
-                load.start()
         for i in range(blocks.shape[0]):
             at = pl.ds(i * blocks.shape[1], blocks.shape[1])
             block_out[at, :] = blocks[i]
@@ -913,75 +911,45 @@
         gain_sum = jnp.sum(gains[...], axis=0)
         gain_attn[...] = gain_sum[0:1, :]
         gain_moe[...] = gain_sum[1:2, :]
-        query[...] = sums_all[:width, :].astype(jnp.float32)
-        pair[...] = sums_all[width : 2 * width, :].astype(jnp.float32)
+        query[...] = sums[:width, :].astype(jnp.float32)
+        pair[...] = sums[width : 2 * width, :].astype(jnp.float32)
         for i in range(width // LANES):
             at = slice(i * LANES, (i + 1) * LANES)
             output[:, at] = output_all[at, :].astype(jnp.float32)
-        router[...] = sums_all[2 * width : 2 * width + router.shape[0], :].astype(jnp.float32)
-
-    expert = picked(order, step)
+        router[...] = sums[2 * width : 2 * width + router.shape[0], :].astype(jnp.float32)
+
     first = 0
     for count, in_sum, out_sum in zip(counts, in_sums, out_sums):
 
-        @pl.when((expert >= first) & (expert < first + count))
+        @pl.when((step >= first) & (step < first + count))
         def _(in_sum=in_sum, out_sum=out_sum):
             gout[0] = out_sum[0].astype(jnp.float32)
-            widened(in_sum.at[0], gin)
+            widened(in_sum.at[0], gin.at[0])
 
         first += count
-    if late:
-
-        @pl.when(expert >= first)
-        def _():
-            @pl.when(expert == first)
-            def _():
-                for load in sums.loads(*work[4:]):
-                    load.wait()
-                sums.ready()
-
-            index = lax.axis_index("row") * len(order) + expert
-            gout[0] = sums.make(index, work[0][0], work[1][0], *work[2:4])
-            widened(sums.turned, gin)
-
-
-def outputs(in_sums, out_sums, work, blocks, in_blocks, gains, sums, output_all, experts):
-    w_out, grads_far = work[1], work[5]
-    total, hidden, width = w_out.shape
-    layers, _, tokens = grads_far.shape
+
+
+def outputs(in_sums, out_sums, hidden, blocks, in_blocks, gains, sums, output_all, experts):
     counts = [s.shape[0] for s in in_sums]
-    late = total - sum(counts)
-    order = order_of(total, late)
+    total = sum(counts)
+    width = out_sums[0].shape[2]
     parts = hidden // LANES
     lanes = blocks.shape[2]
+    tokens = blocks.shape[0] * blocks.shape[1]
     once = lambda s: pl.BlockSpec(s, lambda e: (0,) * len(s))
-    each = lambda s: pl.BlockSpec((1,) + s[1:], lambda e: (picked(order, e), 0, 0))
+    each = lambda s: pl.BlockSpec((1,) + s[1:], lambda e: (e, 0, 0))
     specs = []
     for arrays in (in_sums, out_sums):
         first = 0
         for array in arrays:
-            places, last = [], 0
-            for expert in order:
-                if first <= expert < first + array.shape[0]:
-                    last = expert - first
-                elif expert < total - late and expert >= first + array.shape[0]:
-                    last = array.shape[0] - 1
-                places.append(last)
+            count = array.shape[0]
             specs.append(
                 pl.BlockSpec(
-                    (1,) + array.shape[1:], lambda e, places=places: (picked(places, e), 0, 0)
+                    (1,) + array.shape[1:],
+                    lambda e, first=first, count=count: (jnp.clip(e - first, 0, count - 1), 0, 0),
                 )
             )
-            first += array.shape[0]
-    more, scratch = (), []
-    if late:
-        turns, place = [], total - late
-        for expert in order:
-            turns.append(place)
-            place = min(place + (expert >= total - late), total - 1)
-        ahead = lambda s: pl.BlockSpec((1,) + s[1:], lambda e: (picked(turns, e), 0, 0))
-        more = work
-        scratch = sums_scratch(layers, tokens, width, hidden)
+            first += count
     full = jnp.float32
     shapes = [
         ((total, width * 2 * parts, LANES), full),
@@ -997,17 +965,13 @@
     ]
     small = (blocks, in_blocks, gains, sums, output_all)
     gin, *others = pl.pallas_call(
-        functools.partial(outputs_body, counts, order),
+        functools.partial(outputs_body, counts),
         grid=(total,),
-        in_specs=specs
-        + [once(a.shape) for a in small]
-        + [ahead(a.shape) for a in more[:4]]
-        + [HBM for _ in more[4:]],
+        in_specs=specs + [once(a.shape) for a in small],
         out_specs=(each(shapes[0][0]), each(shapes[1][0])) + tuple(once(s) for s, _ in shapes[2:]),
         out_shape=tuple(jax.ShapeDtypeStruct(*shape) for shape in shapes),
-        scratch_shapes=scratch,
         name="outputs",
-    )(*in_sums, *out_sums, *small, *more)
+    )(*in_sums, *out_sums, *small)
     gin = gin.reshape(total, width, parts, 2, LANES).transpose(0, 1, 3, 2, 4)
     return gin.reshape(total, width, 2, hidden), *others
 
@@ -1262,19 +1226,15 @@
     results = [
         ("swap", block_out),
         ("swap", in_grad),
-        ("line", gain_sum, True),
-        ("line", summed, True),
-        ("line", output_summed, True),
+        ("collect", summed),
+        ("collect", output_summed),
+        ("collect", gain_sum),
     ]
-    if depth > 4:
-        moved = beneath("swap_results", 8, *results)
-    else:
-        moved = exchange(sizes, "swap_results", 8, *results)
-    block_out, in_grad, gain_all, sums, output_all = moved
+    block_out, in_grad, sums, output_all, gain_all = beneath("swap_results", 8, *results)
     grad_in, grad_out, block_out, in_grad, gain_attn_sum, gain_moe_sum, query_sum, pair_sum, output_sum, router_sum = outputs(
         in_sums,
         out_sums,
-        work,
+        hidden,
         block_out,
         in_grad,
         gain_all,

time: 270 us -> 246 us (0.911)
  Pallas kernels: 265 us -> 242 us
    pallas_call x3 -> x4, Pallas kernels: 60.2 us -> 80.9 us  [cover(): pl.pallas_call(functools.partial(cover_body, sizes, kinds, experts, first...]
    pallas_call x6 -> x5, Pallas kernels: 90.2 us -> 71 us  [exchange(): pl.pallas_call(functools.partial(exchange_body, sizes, kinds), out_shape=...]
    pallas_call x1, Pallas kernels: 30 us -> 15.8 us  [outputs(): pl.pallas_call(functools.partial(outputs_body, counts), grid=(total,), in...]
    pallas_call x1, Pallas kernels: 49.6 us -> 38.5 us  [local_experts(): pl.pallas_call(functools.partial(local_experts_body, sizes, kinds), grid=...]
where the time goes in v2:
time: 246 us
  Pallas kernels  242 us (98%)
  other arithmetic  3.03 us (1%)
    pallas_call x4, Pallas kernels, cover(): pl.pallas_call(functools.partial(cover_body, sizes, kinds, experts, first...  80.9 us
    pallas_call x5, Pallas kernels, exchange(): pl.pallas_call(functools.partial(exchange_body, sizes, kinds), out_shape=...  71 us
    pallas_call x1, Pallas kernels, local_experts(): pl.pallas_call(functools.partial(local_experts_body, sizes, kinds), grid=...  38.5 us
    pallas_call x7, Pallas kernels, call(): pl.pallas_call(body, out_shape=tuple((jax.ShapeDtypeStruct(*shape) for sh...  35.4 us
    pallas_call x1, Pallas kernels, outputs(): pl.pallas_call(functools.partial(outputs_body, counts), grid=(total,), in...  15.8 us

profile of v2, /device:TPU:0, one launch (start us, length us, event | category | flops | bytes accessed | tf_op | source)
XLA Modules:
  0.0 245.6 jit_solution(2740063520606178686)
XLA Ops:
  0.6 1.2 pad_maximum_fusion.refs_1_
  1.9 1.8 fusion
  3.7 22.4 %gather_tokens.1 = (bf16[8,512,128]{2,1,0:T(8,128)(2,1)}, bf16[8,2,128]{2,1,0:T(2,128)(2,1)}, bf16[8,32,128]{2,1,0:T(8,128)(2,1)}, s32[3,4,128]{2,1,0:T(4,128)},...) custom-call(bf16[512,128]{1,0:T(8,128)(2,1)} %refs_0_.1, bf16[2,128]{1,0:T(2,128)(2,1)} %pad_maximum_fusion.refs_1_, ...), custom_call_target="tpu_custom_call" | custom-call | tf_op jit(solution)/shard_map/gather_tokens/pallas_call | solution.py:299
  26.1 4.4 %project.1 = (bf16[512,1024]{1,0:T(8,128)(2,1)}, bf16[512,128]{1,0:T(8,128)(2,1)}, bf16[512,128]{1,0:T(8,128)(2,1)}, bf16[64,1024]{1,0:T(8,128)(2,1)}, bf16[64,1...) custom-call(bf16[8,512,128]{2,1,0:T(8,128)(2,1)} %get-tuple-element.88.blocks, ...), custom_call_target="tpu_custom_call" | custom-call | tf_op jit(solution)/shard_map/project/pallas_call | solution.py:321
  30.5 14.5 %shift_pairs.1 = (bf16[2,512,128]{2,1,0:T(8,128)(2,1)}, bf16[8,128,1024]{2,1,0:T(8,128)(2,1)}) custom-call(bf16[512,128]{1,0:T(8,128)(2,1)} %get-tuple-element.93.refs_0_.pair, bf16[128,1024]{1,0:T(8,128)(2,1)} %w_output.1), custom_call_target="tpu_custom_call" | custom-call | tf_op jit(solution)/shard_map/shift_pairs/pallas_call | solution.py:299
  45.0 6.5 %attend.1 = (bf16[512,128]{1,0:T(8,128)(2,1)}, f32[1024,1]{1,0:T(8,128)}, s32[512,1]{1,0:T(8,128)}) custom-call(bf16[512,128]{1,0:T(8,128)(2,1)} %get-tuple-element.92.query, bf16[512,128]{1,0:T(8,128)(2,1)} %get-tuple-element.93.refs_0_.pair, bf16[2,512,128]{2,1,0:T(8,128)(2,1)} %get-tuple-element.94.far, s32[4,128]{1,0:T(4,128)} %bitcast.64, ...), custom_call_target="tpu_custom_call" | custom-call | tf_op jit(solution)/shard_map/attend/pallas_call | solution.py:321
  51.5 5.9 %swap_mixed.1.mixed = bf16[8,64,128]{2,1,0:T(8,128)(2,1)} custom-call(bf16[8,64,128]{2,1,0:T(8,128)(2,1)} %bitcast.58), custom_call_target="tpu_custom_call" | custom-call | tf_op jit(solution)/shard_map/swap_mixed/pallas_call | solution.py:299
  57.4 3.9 %middle.1 = (bf16[64,1152]{1,0:T(8,128)(2,1)}, f32[64,1024]{1,0:T(8,128)}, f32[64,128]{1,0:T(8,128)}) custom-call(bf16[8,64,128]{2,1,0:T(8,128)(2,1)} %swap_mixed.1.mixed, bf16[64,1024]{1,0:T(8,128)(2,1)} %get-tuple-element.97.own, bf16[1024,1024]{1,0:T(8,128)(2,1)} %bitcast.48, bf16[8,2,128]{2,1,0:T(2,128)(2,1)} %get-tuple-element.89.gains, ...), custom_call_target="tpu_custom_call" | custom-call | tf_op jit(solution)/shard_map/middle/pallas_call | solution.py:321
  61.3 15.8 %gather_rows.1 = (bf16[8,64,1152]{2,1,0:T(8,128)(2,1)}, bf16[3,64,1152]{2,1,0:T(8,128)(2,1)}) custom-call(bf16[64,1152]{1,0:T(8,128)(2,1)} %get-tuple-element.100.refs_0_.refs_1_, bf16[64,1152]{1,0:T(8,128)(2,1)} %get-tuple-element.100.refs_0_.refs_1_), custom_call_target="tpu_custom_call" | custom-call | tf_op jit(solution)/shard_map/gather_rows/pallas_call | solution.py:299
  77.1 38.5 %local_experts.1 = (bf16[512,1024]{1,0:T(8,128)(2,1)}, bf16[512,1152]{1,0:T(8,128)(2,1)}, bf16[8,1024,512]{2,1,0:T(8,128)(2,1)}, bf16[8,512,1024]{2,1,0:T(8,128)...) custom-call(bf16[512,1152]{1,0:T(8,128)(2,1)} %bitcast.46, ...), custom_call_target="tpu_custom_call" | custom-call | tf_op jit(solution)/shard_map/local_experts/pallas_call | solution.py:714
  115.6 19.3 %swap_back.1 = (bf16[2,4096,128]{2,1,0:T(8,128)(2,1)}, bf16[2,256,1024]{2,1,0:T(8,128)(2,1)}, bf16[8,64,1152]{2,1,0:T(8,128)(2,1)}) custom-call(bf16[8,1024,512]{2,1,0:T(8,128)(2,1)} %get-tuple-element.105.refs_0_, bf16[8,256,1024]{2,1,0:T(8,128)(2,1)} %refs_1_.9, bf16[8,512,1024]{2,1,0:T(8,128)(2,1)} %get-tuple-element.106.refs_2_, ...), custom_call_target="tpu_custom_call" | custom-call | tf_op jit(solution)/shard_map/swap_back/pallas_call | solution.py:881
  134.9 2.7 %middle_back.1 = (f32[64,1024]{1,0:T(8,128)}, bf16[64,1024]{1,0:T(8,128)(2,1)}, bf16[64,128]{1,0:T(8,128)(2,1)}, f32[1,1024]{1,0:T(1,128)}) custom-call(bf16[8,64,1152]{2,1,0:T(8,128)(2,1)} %get-tuple-element.112.back, bf16[64,1024]{1,0:T(8,128)(2,1)} %get-tuple-element.113.out_grad, f32[64,1024]{1,0:T(8,128)} %get-tuple-element.114.middle, ...), custom_call_target="tpu_custom_call" | custom-call | tf_op jit(solution)/shard_map/middle_back/pallas_call | solution.py:321
  137.6 12.3 %gather_attn_grad.1 = (bf16[8,64,1024]{2,1,0:T(8,128)(2,1)}, bf16[8,64,128]{2,1,0:T(8,128)(2,1)}) custom-call(bf16[64,1024]{1,0:T(8,128)(2,1)} %get-tuple-element.116.refs_0_, bf16[64,128]{1,0:T(8,128)(2,1)} %get-tuple-element.117.refs_1_), custom_call_target="tpu_custom_call" | custom-call | tf_op jit(solution)/shard_map/gather_attn_grad/pallas_call | solution.py:299
  150.0 10.4 %attend_back.1 = (bf16[512,128]{1,0:T(8,128)(2,1)}, f32[512,128]{1,0:T(8,128)}, bf16[2,512,128]{2,1,0:T(8,128)(2,1)}, bf16[8,128,128]{2,1,0:T(8,128)(2,1)}) custom-call(bf16[512,1024]{1,0:T(8,128)(2,1)} %bitcast.53, bf16[128,1024]{1,0:T(8,128)(2,1)} %w_output.1, bf16[512,128]{1,0:T(8,128)(2,1)} %get-tuple-element.92.query, ...), custom_call_target="tpu_custom_call" | custom-call | tf_op jit(solution)/shard_map/attend_back/pallas_call | solution.py:321
  160.4 19.4 %shift_grads.1 = (bf16[2,4096,128]{2,1,0:T(8,128)(2,1)}, bf16[2,256,1024]{2,1,0:T(8,128)(2,1)}, bf16[2,512,128]{2,1,0:T(8,128)(2,1)}, bf16[8,64,1024]{2,1,0:T(8,128)(2,1)}, bf16[4,256,128]{2,1,0:T(8,128)(2,1)}) custom-call(bf16[8,1024,512]{2,1,0:T(8,128)(2,1)} %get-tuple-element.105.refs_0_, bf16[8,256,1024]{2,1,0:T(8,128)(2,1)} %refs_1_.9, ...), custom_call_target="tpu_custom_call" | custom-call | tf_op jit(solution)/shard_map/shift_grads/pallas_call | solution.py:881
  179.7 4.4 %project_back.1 = (bf16[512,1024]{1,0:T(8,128)(2,1)}, bf16[2176,128]{1,0:T(8,128)(2,1)}, bf16[256,128]{1,0:T(8,128)(2,1)}, f32[8,8,128]{2,1,0:T(8,128)}) custom-call(bf16[512,128]{1,0:T(8,128)(2,1)} %get-tuple-element.125.query_grad, f32[512,128]{1,0:T(8,128)} %get-tuple-element.126.pair_grad, bf16[2,512,128]{2,1,0:T(8,128)(2,1)} %get-tuple-element.127.returned, ...), custom_call_target="tpu_custom_call" | custom-call | tf_op jit(solution)/shard_map/project_back/pallas_call | solution.py:321
  184.2 19.4 %swap_partial.1 = (bf16[2,4096,128]{2,1,0:T(8,128)(2,1)}, bf16[2,256,1024]{2,1,0:T(8,128)(2,1)}, bf16[8,64,1024]{2,1,0:T(8,128)(2,1)}, bf16[4,544,128]{2,1,0:T(8,128)(2,1)}, f32[8,8,128]{2,1,0:T(8,128)}) custom-call(bf16[8,1024,512]{2,1,0:T(8,128)(2,1)} %get-tuple-element.105.refs_0_, bf16[8,256,1024]{2,1,0:T(8,128)(2,1)} %refs_1_.9, ...), custom_call_target="tpu_custom_call" | custom-call | tf_op jit(solution)/shard_map/swap_partial/pallas_call | solution.py:881
  203.6 3.1 %results.1 = (bf16[8,64,128]{2,1,0:T(8,128)(2,1)}, bf16[8,64,128]{2,1,0:T(8,128)(2,1)}, f32[8,128]{1,0:T(8,128)}, bf16[544,128]{1,0:T(8,128)(2,1)}) custom-call(bf16[8,64,1024]{2,1,0:T(8,128)(2,1)} %get-tuple-element.136.blocks, bf16[8,64,1024]{2,1,0:T(8,128)(2,1)} %get-tuple-element.137.moe, bf16[64,1024]{1,0:T(8,128)(2,1)} %get-tuple-element.97.own, ...), custom_call_target="tpu_custom_call" | custom-call | tf_op jit(solution)/shard_map/results/pallas_call | solution.py:321
  206.7 22.9 %swap_results.1 = (bf16[2,4096,128]{2,1,0:T(8,128)(2,1)}, bf16[2,256,1024]{2,1,0:T(8,128)(2,1)}, bf16[8,64,128]{2,1,0:T(8,128)(2,1)}, bf16[8,64,128]{2,1,0:T(8,1...) custom-call(bf16[8,1024,512]{2,1,0:T(8,128)(2,1)} %get-tuple-element.105.refs_0_, ...), custom_call_target="tpu_custom_call" | custom-call | tf_op jit(solution)/shard_map/swap_results/pallas_call | solution.py:881
  229.6 15.8 %outputs.1 = (f32[8,4096,128]{2,1,0:T(8,128)}, f32[8,256,1024]{2,1,0:T(8,128)}, bf16[512,128]{1,0:T(8,128)(2,1)}, bf16[512,128]{1,0:T(8,128)(2,1)}, f32[1,128]{1...) custom-call(bf16[2,4096,128]{2,1,0:T(8,128)(2,1)} %get-tuple-element, ...), custom_call_target="tpu_custom_call" | custom-call | tf_op jit(solution)/shard_map/outputs/pallas_call | solution.py:967
  (2 shorter events, 0.0 us)
